TPU v7x, 32 devices: a whole 2x2x4 slice. The times are simulated.
32 devices in a mesh: section: 4 (over y, core), expert: 8 (over z, x).
Axes of the slice: x: 2, y: 2, z: 4, core: 2. Of those that a mesh axis runs over, the one named last changes fastest.
Arguments:
- inputs: bfloat16 [4, 1024, 1024], P('section', 'expert'), may hold values from -6 to 6
- out_grads: bfloat16 [4, 1024, 1024], P('section', 'expert'), may hold values from -6 to 6
- expert_ids: int32 [4, 1024, 8], P('section', 'expert'), may hold values from 0 to 15, all different within a row; in each aligned block of 128 rows (0 to 127, 128 to 255, ..., all dimensions but the last counted through in order) at most 96 rows name the same one
- route_levels: int32 [4, 1024, 8], P('section', 'expert'), may hold values from 8 to 256
- w_gate: bfloat16 [4, 16, 1024, 384], P('section', 'expert'), may hold values from -0.1875 to 0.1875
- w_up: bfloat16 [4, 16, 1024, 384], P('section', 'expert'), may hold values from -0.1875 to 0.1875
- w_down: bfloat16 [4, 16, 384, 1024], P('section', 'expert'), may hold values from -0.3125 to 0.3125
Outputs:
- upstream: bfloat16 [4, 1024, 1024], P('section', 'expert')
- route_grad: bfloat16 [4, 1024, 8], P('section', 'expert')
- gate_update: bfloat16 [4, 16, 1024, 384], P('section', 'expert')
- up_update: bfloat16 [4, 16, 1024, 384], P('section', 'expert')
- down_update: bfloat16 [4, 16, 384, 1024], P('section', 'expert')
Inputs may be any that keep to these rules, and one draw needn't show every extreme that they name: `expert_ids`: each token names 8 different experts; among the 128 tokens of one aligned block no expert is named more than 96 times.
All inputs are finite; a program needn't handle non-finite values.
Results may differ from a plain program's by a relative error of at most 0.0064.
Values may be sent and summed in bfloat16 or wider, within the bound.
No kernel may reach another device: no remote copies, remote signals or barrier semaphores. Data moves between devices by JAX's collectives and lax.ppermute only.
A program may use at most 128 MiB of HBM per device.

v0:
```python
import jax
import jax.numpy as jnp
from jax import lax
from jax.sharding import PartitionSpec as P


def shifted(value, axis, by):
    size = lax.axis_size(axis)
    pairs = [(i, i + by) for i in range(size) if 0 <= i + by < size]
    return lax.ppermute(value, axis, pairs)


def flat_slots(expert_ids, experts_all, capacity):
    blocks = expert_ids.shape[0]
    flat_ids = expert_ids.reshape(blocks, -1)
    catalog = jnp.arange(experts_all, dtype=jnp.int32)
    onehot = (flat_ids[:, :, None] == catalog[None, None, :]).astype(jnp.int32)
    rank_table = jnp.cumsum(onehot, axis=1) - 1
    slot_of = jnp.sum(onehot * rank_table, axis=2)
    return (flat_ids * capacity + slot_of).reshape(expert_ids.shape)


def expert_backward(slot_inputs, slot_grads, slot_routes, w_gate, w_up, w_down):
    gate_pre = jnp.einsum("esd,edh->esh", slot_inputs, w_gate, preferred_element_type=jnp.float32)
    up_pre = jnp.einsum("esd,edh->esh", slot_inputs, w_up, preferred_element_type=jnp.float32)
    sigmoid_gate = jax.nn.sigmoid(gate_pre)
    silu_gate = gate_pre * sigmoid_gate
    active = (silu_gate * up_pre).astype(jnp.bfloat16)
    expert_out = jnp.einsum("esh,ehd->esd", active, w_down, preferred_element_type=jnp.float32)
    route_part = jnp.sum(slot_grads.astype(jnp.float32) * expert_out, axis=2).astype(jnp.bfloat16)
    weighted = (
        slot_routes.astype(jnp.float32)[:, :, None] * slot_grads.astype(jnp.float32)
    ).astype(jnp.bfloat16)
    active_grad = jnp.einsum("esd,ehd->esh", weighted, w_down, preferred_element_type=jnp.float32)
    gate_pre_grad = (
        active_grad * up_pre * sigmoid_gate * (1.0 + gate_pre * (1.0 - sigmoid_gate))
    ).astype(jnp.bfloat16)
    up_pre_grad = (active_grad * silu_gate).astype(jnp.bfloat16)
    input_grad = (
        jnp.einsum("esh,edh->esd", gate_pre_grad, w_gate, preferred_element_type=jnp.float32)
        + jnp.einsum("esh,edh->esd", up_pre_grad, w_up, preferred_element_type=jnp.float32)
    ).astype(jnp.bfloat16)
    down_part = jnp.einsum(
        "esh,esd->ehd", active, weighted, preferred_element_type=jnp.float32
    ).astype(jnp.bfloat16)
    gate_part = jnp.einsum(
        "esd,esh->edh", slot_inputs, gate_pre_grad, preferred_element_type=jnp.float32
    ).astype(jnp.bfloat16)
    up_part = jnp.einsum(
        "esd,esh->edh", slot_inputs, up_pre_grad, preferred_element_type=jnp.float32
    ).astype(jnp.bfloat16)
    return (input_grad, route_part, gate_part, up_part, down_part)


def body(inputs, out_grads, expert_ids, route_levels, w_gate, w_up, w_down):
    tok_rows = inputs.shape[1]
    width = inputs.shape[2]
    top_count = expert_ids.shape[2]
    experts_local = w_gate.shape[1]
    groups = lax.axis_size("expert")
    experts_all = experts_local * groups
    capacity = 3 * tok_rows * top_count // (2 * experts_all)
    slot_total = experts_all * capacity
    own_index = flat_slots(expert_ids[0][None], experts_all, capacity)[0]
    catalog = jnp.arange(slot_total, dtype=jnp.int32)
    select = (own_index[:, :, None] == catalog).astype(jnp.bfloat16)
    placing = jnp.sum(select, axis=1)
    route_values = (route_levels[0].astype(jnp.float32) / 256.0).astype(jnp.bfloat16)
    all_inputs, all_grads, all_routes, all_choices = (
        lax.all_gather(inputs[0], "expert", axis=0, tiled=True),
        lax.all_gather(out_grads[0], "expert", axis=0, tiled=True),
        lax.all_gather(route_values, "expert", axis=0, tiled=True),
        lax.all_gather(expert_ids[0].astype(jnp.bfloat16), "expert", axis=0, tiled=True),
    )
    source_ids = all_choices.astype(jnp.int32).reshape(groups, tok_rows, top_count)
    first_expert = lax.axis_index("expert") * experts_local
    local_index = flat_slots(source_ids, experts_all, capacity) - first_expert * capacity
    local_catalog = jnp.arange(experts_local * capacity, dtype=jnp.int32)
    local_select = (
        (local_index[..., None] == local_catalog)
        .astype(jnp.bfloat16)
        .reshape(groups, tok_rows, top_count, experts_local, capacity)
    )
    local_placing = jnp.sum(local_select, axis=2)
    slot_inputs = (
        jnp.einsum(
            "ntec,ntd->encd",
            local_placing,
            all_inputs.reshape(groups, tok_rows, width),
            preferred_element_type=jnp.float32,
        )
        .astype(jnp.bfloat16)
        .reshape(experts_local, groups * capacity, width)
    )
    slot_grads = (
        jnp.einsum(
            "ntec,ntd->encd",
            local_placing,
            all_grads.reshape(groups, tok_rows, width),
            preferred_element_type=jnp.float32,
        )
        .astype(jnp.bfloat16)
        .reshape(experts_local, groups * capacity, width)
    )
    slot_routes = (
        jnp.einsum(
            "ntkec,ntk->enc",
            local_select,
            all_routes.reshape(groups, tok_rows, top_count),
            preferred_element_type=jnp.float32,
        )
        .astype(jnp.bfloat16)
        .reshape(experts_local, groups * capacity)
    )
    input_grad, route_part, gate_part, up_part, down_part = expert_backward(
        slot_inputs, slot_grads, slot_routes, w_gate[0], w_up[0], w_down[0]
    )
    back_inputs, back_routes = (
        lax.all_to_all(input_grad, "expert", split_axis=1, concat_axis=0, tiled=True),
        lax.all_to_all(route_part, "expert", split_axis=1, concat_axis=0, tiled=True),
    )
    token_grad = jnp.dot(
        placing, back_inputs.reshape(slot_total, width), preferred_element_type=jnp.float32
    ).astype(jnp.bfloat16)
    token_route = jnp.einsum(
        "tks,s->tk", select, back_routes.reshape(slot_total), preferred_element_type=jnp.float32
    ).astype(jnp.bfloat16)
    upstream = shifted(token_grad, "section", -1)
    return (upstream[None], token_route[None], gate_part[None], up_part[None], down_part[None])


def solution(mesh):
    in_specs = (
        P("section", "expert", None),
        P("section", "expert", None),
        P("section", "expert", None),
        P("section", "expert", None),
        P("section", "expert", None, None),
        P("section", "expert", None, None),
        P("section", "expert", None, None),
    )
    out_specs = (
        P("section", "expert", None),
        P("section", "expert", None),
        P("section", "expert", None, None),
        P("section", "expert", None, None),
        P("section", "expert", None, None),
    )
    return jax.shard_map(body, mesh=mesh, in_specs=in_specs, out_specs=out_specs, check_vma=False)
```

profile of v0, /device:TPU:1, one launch (start us, length us, event | category | flops | bytes accessed | tf_op | source)
XLA Modules:
  0.0 240.5 jit_solution(3943738356832630842)
XLA Ops:
  9.4 23.1 %all-gather.1 = bf16[1,1024,8]{1,2,0:T(8,128)(2,1)S(1)} all-gather(bf16[1,128,8]{1,2,0:T(8,128)(2,1)S(1)} %convert_element_type.122), channel_id=3, replica_groups=mesh['section'=4,'expert'=8] {'expert'}, dimensions={1}, use_global_device_ids=true | all-gather | bytes 18432 | tf_op jit(solution)/shard_map/all_gather | solution.py:73
  33.4 36.0 %reduce-window.16 = s32[8,16,8,128]{3,2,1,0:T(8,128)S(1)} reduce-window(s32[8,16,8,128]{3,2,1,0:T(8,128)S(1)} %fusion.23, s32[]{:T(128)} %constant.30.clone.1), window={size=1x1x1x128 pad=0_0x0_0x0_0x127_0}, to_apply=%region_4.5 | reduce-window | flops 16646144 | bytes 1048580 | tf_op jit(solution)/shard_map/reduce-window.2
  71.2 22.5 %all-gather = bf16[1,1024,8]{1,2,0:T(8,128)(2,1)S(1)} all-gather(bf16[1,128,8]{1,2,0:T(8,128)(2,1)S(1)} %multiply_convert_fusion.3), channel_id=2, replica_groups=mesh['section'=4,'expert'=8] {'expert'}, dimensions={1}, use_global_device_ids=true | all-gather | bytes 18432 | tf_op jit(solution)/shard_map/all_gather | solution.py:72
  93.7 1.1 fusion.4
  95.0 0.7 convert_reduce_fusion
  95.7 2.6 %convert_bitcast_fusion.1 = bf16[2,8,96,1024]{3,2,0,1:T(8,128)(2,1)S(1)} fusion(bf16[8,128,2,96]{1,3,2,0:T(8,128)(2,1)S(1)} %convert_reduce_fusion, bf16[8,128,1024,1]{2,1,3,0:T(8,128)(2,1)} %bitcast.118), kind=kOutput, calls=%fused_computation.12 | convolution fusion | flops 404226048 | bytes 5636096 | tf_op jit(solution)/shard_map/ntec,ntd->encd/dot_general | solution.py:86
  98.3 2.1 copy.95
  100.4 10.0 %all-gather.7.cloned.1.call-done = bf16[1,1024,1024]{2,1,0:T(8,128)(2,1)} async-done(((bf16[1,128,1024]{2,1,0:T(8,128)(2,1)}), bf16[1,1024,1024]{2,1,0:T(8,128)(2,1)}) %all-gather.7.cloned.1.call-update) | async-done | bytes 2097168 | tf_op jit(solution)/shard_map/all_gather | solution.py:71
  110.4 2.6 %convert_bitcast_fusion = f32[2,8,96,1024]{3,2,0,1:T(8,128)S(1)} fusion(bf16[8,128,2,96]{1,3,2,0:T(8,128)(2,1)S(1)} %convert_reduce_fusion, bf16[8,128,1024,1]{2,1,3,0:T(8,128)(2,1)} %bitcast.112), kind=kOutput, calls=%fused_computation.4 | convolution fusion | flops 405798912 | bytes 8781824 | tf_op jit(solution)/shard_map/ntec,ntd->encd/dot_general | solution.py:96
  112.9 1.1 copy.94
  114.1 0.7 copy-done.1
  115.3 1.8 fusion.11
  117.5 1.0 copy-done.4
  118.5 1.8 fusion.17
  120.3 4.2 %multiply_convert_fusion = (bf16[2,768,384]{2,1,0:T(8,128)(2,1)S(1)}, bf16[2,768,384]{2,1,0:T(8,128)(2,1)}, bf16[2,768,384]{2,1,0:T(8,128)(2,1)}) fusion(f32[2,768,384]{2,1,0:T(8,128)S(1)} %fusion.11, f32[2,768,384]{2,1,0:T(8,128)S(1)} %fusion.17, bf16[2,768,1024]{2,1,0:T(8,128)(2,1)S(1)} %bitcast.114, bf16[1,2,1024,384]{3,2,1,0:T(8,128)(2,1)S(1)} %copy-done), kind=kOutput, calls=%fused_computation.16 | convolution fusion | flops 1216806912 | bytes 12976128 | tf_op jit(solution)/shard_map/esd,edh->esh/dot_general | solution.py:25
  124.5 1.0 copy-done.9
  125.5 1.9 fusion.1
  128.1 3.7 %all-to-all-start.1 = ((bf16[2,8,96]{2,0,1:T(2,128)(2,1)}), bf16[2,8,96]{2,0,1:T(2,128)(2,1)S(1)}, u32[]{:S(2)}, u32[]{:S(2)}) async-start(bf16[2,8,96]{2,0,1:T(2,128)(2,1)} %copy.99), calls=%async_computation.1 | async-start | bytes 8192 | tf_op jit(solution)/shard_map/all_to_all | solution.py:120
  131.8 3.2 %fusion.9 = f32[2,768,1024]{2,1,0:T(8,128)S(1)} fusion(bf16[2,768,384]{2,1,0:T(8,128)(2,1)} %get-tuple-element.6, bf16[1,2,1024,384]{3,2,1,0:T(8,128)(2,1)S(1)} %copy-done.5), kind=kOutput, calls=%fused_computation.24 | convolution fusion | flops 1207959552 | bytes 9043968 | tf_op jit(solution)/shard_map/esh,edh->esd/dot_general | solution.py:40
  135.0 1.8 add_convert_fusion
  136.9 4.9 %copy.96 = bf16[2,768,1024]{2,0,1:T(2,128)(2,1)} copy(bf16[2,768,1024]{2,1,0:T(8,128)(2,1)S(1)} %add_convert_fusion) | data formatting | bytes 6291456 | tf_op jit(solution)/shard_map/convert_element_type | solution.py:42
  141.8 5.6 %all-to-all-start = ((bf16[2,768,1024]{2,0,1:T(2,128)(2,1)}), bf16[2,768,1024]{2,0,1:T(2,128)(2,1)}, u32[]{:S(2)}, u32[]{:S(2)}) async-start(bf16[2,768,1024]{2,0,1:T(2,128)(2,1)} %copy.96), calls=%async_computation | async-start | bytes 6291456 | tf_op jit(solution)/shard_map/all_to_all | solution.py:119
  147.6 4.5 %reduce-window.14 = s32[1,16,8,128]{3,2,1,0:T(8,128)S(1)} reduce-window(s32[1,16,8,128]{3,2,1,0:T(8,128)S(1)} %bitcast.120, s32[]{:T(128)} %constant.30.clone.1), window={size=1x1x1x128 pad=0_0x0_0x0_0x127_0}, to_apply=%region_0.0 | reduce-window | flops 2080768 | bytes 131076 | tf_op jit(solution)/shard_map/reduce-window
  152.7 3.1 %fusion.6 = bf16[128,1536]{1,0:T(8,128)(2,1)S(1)} fusion(s32[128,8]{1,0:T(8,128)S(1)} %bitcast_add_fusion), kind=kLoop, calls=%fused_computation.11 | loop fusion | flops 4521984 | bytes 397312 | tf_op jit(solution)/shard_map/reduce_sum | solution.py:67
  155.9 4.6 %fusion.21 = bf16[1,2,384,1024]{3,2,1,0:T(8,128)(2,1)} fusion(bf16[2,768,384]{2,1,0:T(8,128)(2,1)S(1)} %copy-done.10, bf16[2,768,1024]{2,1,0:T(8,128)(2,1)} %copy-done.3), kind=kOutput, calls=%fused_computation.36 | convolution fusion | flops 1208745984 | bytes 5898240 | tf_op jit(solution)/shard_map/esh,esd->ehd/dot_general | solution.py:43
  160.5 3.0 %fusion.19 = bf16[1,2,1024,384]{3,2,1,0:T(8,128)(2,1)} fusion(bf16[2,768,1024]{2,1,0:T(8,128)(2,1)S(1)} %bitcast.115, bf16[2,768,384]{2,1,0:T(8,128)(2,1)S(1)} %copy-done.8), kind=kOutput, calls=%fused_computation.34 | convolution fusion | flops 1208745984 | bytes 5898240 | tf_op jit(solution)/shard_map/esd,esh->edh/dot_general | solution.py:46
  163.5 3.0 %fusion.20 = bf16[1,2,1024,384]{3,2,1,0:T(8,128)(2,1)} fusion(bf16[2,768,1024]{2,1,0:T(8,128)(2,1)S(1)} %bitcast.116, bf16[2,768,384]{2,1,0:T(8,128)(2,1)S(1)} %copy-done.7), kind=kOutput, calls=%fused_computation.35 | convolution fusion | flops 1208745984 | bytes 5898240 | tf_op jit(solution)/shard_map/esd,esh->edh/dot_general | solution.py:49
  166.6 49.5 %all-to-all-done = bf16[2,768,1024]{2,0,1:T(2,128)(2,1)} async-done(((bf16[2,768,1024]{2,0,1:T(2,128)(2,1)}), bf16[2,768,1024]{2,0,1:T(2,128)(2,1)}, u32[]{:S(2)}, u32[]{:S(2)}) %all-to-all-start) | async-done | bytes 3145760 | tf_op jit(solution)/shard_map/all_to_all | solution.py:119
  216.1 2.8 %copy.97 = bf16[2,768,1024]{2,1,0:T(8,128)(2,1)S(1)} copy(bf16[2,768,1024]{2,0,1:T(2,128)(2,1)} %all-to-all-done) | data formatting | bytes 6291456 | tf_op jit(solution)/shard_map/all_to_all | solution.py:119
  219.9 5.2 %collective-permute-start = (bf16[128,1024]{1,0:T(8,128)(2,1)S(1)}, bf16[128,1024]{1,0:T(8,128)(2,1)S(1)}, u32[]{:S(2)}, u32[]{:S(2)}) collective-permute-start(bf16[128,1024]{1,0:T(8,128)(2,1)S(1)} %convolution_convert_fusion.3), channel_id=1, source_target_pairs={{8,0},{16,8},{24,16},{9,1},{17,9},{25,17},{10,2},{18,10},{26,18},{... | collective-permute-start | bytes 786440 | tf_op jit(solution)/shard_map/ppermute | solution.py:10
  225.2 7.1 %fusion.2 = bf16[1,128,8]{2,0,1:T(2,128)(2,1)S(1)} fusion(bf16[1536,1,1]{0,1,2:T(2,128)(2,1)S(1)} %reshape.250, s32[128,8]{1,0:T(8,128)S(1)} %bitcast_add_fusion), kind=kOutput, calls=%fused_computation.7 | convolution fusion | flops 4718592 | bytes 9216 | tf_op jit(solution)/shard_map/tks,s->tk/dot_general | solution.py:125
  232.9 0.7 copy.121
  (76 shorter events, 9.1 us)
Async XLA Ops:
  7.2 113.1 %copy-start = (bf16[1,2,1024,384]{3,2,1,0:T(8,128)(2,1)S(1)}, bf16[1,2,1024,384]{3,2,1,0:T(8,128)(2,1)}, u32[]{:S(2)}) copy-start(bf16[1,2,1024,384]{3,2,1,0:T(8,128)(2,1)} %param.12) | copy-start | bytes 4718596
  7.2 88.5 %all-gather.9.cloned.1.call-start = ((), (), s32[]{:S(2)}) async-start(), calls=%async_computation.3 | async-start | bytes 2359296 | tf_op jit(solution)/shard_map/all_gather | solution.py:70
  7.9 102.4 %all-gather.7.cloned.1.call-start = ((), (), s32[]{:S(2)}) async-start(), calls=%async_computation.2 | async-start | bytes 2359296 | tf_op jit(solution)/shard_map/all_gather | solution.py:71
  70.5 0.8 copy-start.12
  112.9 1.9 copy-start.1
  112.9 2.3 copy-start.5
  117.1 1.4 copy-start.4
  118.5 1.8 copy-start.3
  124.5 1.0 copy-start.9
  128.1 13.7 %all-to-all-start.1 = ((bf16[2,8,96]{2,0,1:T(2,128)(2,1)}), bf16[2,8,96]{2,0,1:T(2,128)(2,1)S(1)}, u32[]{:S(2)}, u32[]{:S(2)}) async-start(bf16[2,8,96]{2,0,1:T(2,128)(2,1)} %copy.99), calls=%async_computation.1 | async-start | bytes 8192 | tf_op jit(solution)/shard_map/all_to_all | solution.py:120
  131.8 3.2 %copy-start.6 = (bf16[2,768,384]{2,1,0:T(8,128)(2,1)S(1)}, bf16[2,768,384]{2,1,0:T(8,128)(2,1)}, u32[]{:S(2)}) copy-start(bf16[2,768,384]{2,1,0:T(8,128)(2,1)} %get-tuple-element.7) | copy-start | bytes 3538948
  141.8 5.6 %copy-start.11 = (s32[1,128,8]{1,2,0:T(8,128)S(1)}, s32[1,128,8]{1,2,0:T(8,128)}, u32[]{:S(2)}) copy-start(s32[1,128,8]{1,2,0:T(8,128)} %param.9) | copy-start | bytes 12292
  141.8 14.1 %copy-start.10 = (bf16[2,768,384]{2,1,0:T(8,128)(2,1)S(1)}, bf16[2,768,384]{2,1,0:T(8,128)(2,1)}, u32[]{:S(2)}) copy-start(bf16[2,768,384]{2,1,0:T(8,128)(2,1)} %copy-done.9) | copy-start | bytes 3538948
  141.8 74.3 %all-to-all-start = ((bf16[2,768,1024]{2,0,1:T(2,128)(2,1)}), bf16[2,768,1024]{2,0,1:T(2,128)(2,1)}, u32[]{:S(2)}, u32[]{:S(2)}) async-start(bf16[2,768,1024]{2,0,1:T(2,128)(2,1)} %copy.96), calls=%async_computation | async-start | bytes 6291456 | tf_op jit(solution)/shard_map/all_to_all | solution.py:119
  155.9 4.6 %copy-start.2 = (bf16[2,8,96,1024]{3,2,1,0:T(8,128)(2,1)S(1)}, bf16[2,8,96,1024]{3,2,1,0:T(8,128)(2,1)}, u32[]{:S(2)}) copy-start(bf16[2,8,96,1024]{3,2,1,0:T(8,128)(2,1)} %copy.95) | copy-start | bytes 9437188
  155.9 4.6 %copy-start.8 = (bf16[2,768,384]{2,1,0:T(8,128)(2,1)S(1)}, bf16[2,768,384]{2,1,0:T(8,128)(2,1)}, u32[]{:S(2)}) copy-start(bf16[2,768,384]{2,1,0:T(8,128)(2,1)} %get-tuple-element.6) | copy-start | bytes 3538948
  160.5 3.0 %copy-start.7 = (bf16[2,768,384]{2,1,0:T(8,128)(2,1)S(1)}, bf16[2,768,384]{2,1,0:T(8,128)(2,1)}, u32[]{:S(2)}) copy-start(bf16[2,768,384]{2,1,0:T(8,128)(2,1)} %get-tuple-element.7) | copy-start | bytes 3538948
  219.9 13.0 %collective-permute-start = (bf16[128,1024]{1,0:T(8,128)(2,1)S(1)}, bf16[128,1024]{1,0:T(8,128)(2,1)S(1)}, u32[]{:S(2)}, u32[]{:S(2)}) collective-permute-start(bf16[128,1024]{1,0:T(8,128)(2,1)S(1)} %convolution_convert_fusion.3), channel_id=1, source_target_pairs={{8,0},{16,8},{24,16},{9,1},{17,9},{25,17},{10,2},{18,10},{26,18},{... | collective-permute-start | bytes 786440 | tf_op jit(solution)/shard_map/ppermute | solution.py:10
Sparse Core Ops, SparseCore 0:
  10.1 50.0 all-gather.8
  62.3 47.9 all-gather.6
where the time goes:
time: 241 us; the launch traced here: 240 us
  waiting for transfers between devices  60.9 us (25%)
  other arithmetic  46 us (19%)
  blocking collectives  45.6 us (19%)
  matrix products  39.2 us (16%)
  local copies, waits for them, and re-layouts  19.8 us (8%)
  starting transfers between devices  14.6 us (6%)
  between operations  14.4 us (6%)
    all_to_all x1, waiting for transfers between devices, body(): lax.all_to_all(input_grad, 'expert', split_axis=1, concat_axis=0, tiled=T...  49.5 us
    another operation x4, other arithmetic  40.6 us
    all_gather x1, blocking collectives, body(): lax.all_gather(expert_ids[0].astype(jnp.bfloat16), 'expert', axis=0, tile...  23.1 us
    all_gather x1, blocking collectives, body(): lax.all_gather(route_values, 'expert', axis=0, tiled=True)  22.5 us
    all_gather x1, waiting for transfers between devices, body(): lax.all_gather(out_grads[0], 'expert', axis=0, tiled=True)  9.99 us
    dot_general x1, matrix products, body(): jnp.einsum('tks,s->tk', select, back_routes.reshape(slot_total), preferre...  7.06 us
    all_to_all x1, starting transfers between devices, body(): lax.all_to_all(input_grad, 'expert', split_axis=1, concat_axis=0, tiled=T...  5.56 us
    ppermute x1, starting transfers between devices, shifted(): return lax.ppermute(value, axis, pairs)  5.24 us
  transfers between devices with their start and end apart: 5, of which 2 were waited for; matrix products, arithmetic and copies ran while one was open for 34% of the time, Pallas kernels for 0%

commit v1 on v0

v1 whole, which is shorter than its diff:
```python
import jax
import jax.numpy as jnp
from jax import lax
from jax.sharding import PartitionSpec as P

F32 = jnp.float32
BF16 = jnp.bfloat16


def ring_order(size):
    columns = 1
    while (2 * columns) ** 2 <= size and size % (2 * columns) == 0:
        columns *= 2
    rows = size // columns
    if columns == 1:
        return list(range(size))
    cells = [(0, 0)]
    for column in range(columns):
        span = range(1, rows) if column % 2 == 0 else range(rows - 1, 0, -1)
        cells += [(row, column) for row in span]
    cells += [(0, column) for column in range(columns - 1, 0, -1)]
    return [row * columns + column for row, column in cells]


def shifted(value, axis, by):
    size = lax.axis_size(axis)
    pairs = [(i, i + by) for i in range(size) if 0 <= i + by < size]
    return lax.ppermute(value, axis, pairs)


def block_backward(x, g, routes, w_in, w_down, experts_local):
    hidden = w_down.shape[0]
    each = hidden // experts_local
    pre = jnp.dot(x, w_in, preferred_element_type=F32)
    gate, up = pre[:, :hidden], pre[:, hidden:]
    back = lax.dot_general(g, w_down, (((1,), (1,)), ((), ())), preferred_element_type=F32)
    lane = lax.broadcasted_iota(jnp.int32, back.shape, 1) // each
    route = jnp.zeros(back.shape, F32)
    for e in range(experts_local):
        route = jnp.where(lane == e, routes[:, e][:, None], route)
    sig = jax.nn.sigmoid(gate)
    silu = gate * sig
    active = (silu * up).astype(BF16).astype(F32)
    scaled = (route * active).astype(BF16)
    grad = route * back
    gate_grad = (grad * up * sig * (1.0 + gate * (1.0 - sig))).astype(BF16)
    up_grad = (grad * silu).astype(BF16)
    product = active * back
    route_grad = jnp.stack(
        [jnp.sum(product[:, e * each:(e + 1) * each], axis=1) for e in range(experts_local)], axis=1
    )
    pre_grad = jnp.concatenate([gate_grad, up_grad], axis=1)
    part = lax.dot_general(pre_grad, w_in, (((1,), (1,)), ((), ())), preferred_element_type=F32)
    return part.astype(BF16), route_grad, pre_grad, scaled


def body(inputs, out_grads, expert_ids, route_levels, w_gate, w_up, w_down):
    x0, g0 = inputs[0], out_grads[0]
    ids = expert_ids[0]
    tokens, width = x0.shape
    experts_local, _, each = w_gate.shape[1:]
    groups = lax.axis_size("expert")
    experts_all = experts_local * groups
    half = groups // 2
    ring = ring_order(groups)
    fwd = [(ring[p], ring[(p + 1) % groups]) for p in range(groups)]
    bwd = [(b, a) for a, b in fwd]

    def go(value, pairs):
        return lax.ppermute(value, "expert", pairs)

    levels = route_levels[0].astype(F32) / 256.0
    catalog = jnp.arange(experts_all, dtype=jnp.int32)
    chosen = ids.T[None, :, :] == catalog[:, None, None]
    table = jnp.sum(jnp.where(chosen, levels.T[None], 0.0), axis=1).astype(BF16)
    received = lax.all_to_all(
        table.reshape(groups, experts_local, tokens), "expert", split_axis=0, concat_axis=0, tiled=True
    )
    ring_arr = jnp.array(ring, jnp.int32)
    me = lax.axis_index("expert")
    place = jnp.sum(jnp.where(ring_arr == me, jnp.arange(groups), 0))
    seat = jnp.sum(
        jnp.where(ring_arr[None, :] == jnp.arange(groups)[:, None], jnp.arange(groups)[None, :], 0), axis=1
    )
    turn = (
        jnp.mod(seat[None, :] - place, groups) == jnp.arange(groups)[:, None]
    ).astype(BF16)
    routes = jnp.dot(turn, received.reshape(groups, -1), preferred_element_type=F32)
    routes = routes.reshape(groups * experts_local, tokens).T

    w_in = jnp.concatenate(
        [w_gate[0, e] for e in range(experts_local)] + [w_up[0, e] for e in range(experts_local)], axis=1
    )
    w_out = w_down[0].reshape(experts_local * each, width)

    xs, gs = {0: x0}, {0: g0}
    xf = xb = x0
    gf = gb = g0
    for hop in range(1, half + 1):
        xf = go(xf, fwd)
        gb = go(gb, bwd)
        xs[groups - hop], gs[hop] = xf, gb
        if hop < half:
            gf = go(gf, fwd)
            xb = go(xb, bwd)
            gs[groups - hop], xs[hop] = gf, xb

    parts, route_grads, pre_grads, scaleds = {}, {}, {}, {}
    order = [0]
    for hop in range(1, half + 1):
        order += [hop] if hop == groups - hop else [hop, groups - hop]
    for o in order:
        mine = routes[:, o * experts_local:(o + 1) * experts_local]
        parts[o], route_grads[o], pre_grads[o], scaleds[o] = lax.optimization_barrier(
            block_backward(xs[o], gs[o], mine, w_in, w_out, experts_local)
        )

    cut = tokens // 2
    low = {o: parts[o][:cut] for o in parts}
    high = {o: parts[o][cut:] for o in parts}

    def chain(pieces, pairs, offsets):
        carried = None
        for o in offsets:
            piece = pieces[o]
            if carried is not None:
                piece = (carried.astype(F32) + piece.astype(F32)).astype(BF16)
            carried = go(piece, pairs)
        return carried

    longer = list(range(half, 0, -1))
    forward_low = chain(low, fwd, longer)
    backward_high = chain(high, bwd, [groups - o for o in longer])
    forward_high = chain(high, fwd, longer[1:])
    backward_low = chain(low, bwd, [groups - o for o in longer[1:]])

    def total(own, one, two):
        return (own.astype(F32) + one.astype(F32) + two.astype(F32)).astype(BF16)

    upstream = jnp.concatenate(
        [
            shifted(total(low[0], forward_low, backward_low), "section", -1),
            shifted(total(high[0], forward_high, backward_high), "section", -1),
        ],
        axis=0,
    )

    back_table = jnp.concatenate([route_grads[o] for o in range(groups)], axis=1).T.astype(BF16)
    back_table = lax.dot_general(
        turn, back_table.reshape(groups, -1), (((0,), (0,)), ((), ())), preferred_element_type=F32
    ).astype(BF16)
    returned = lax.all_to_all(
        back_table.reshape(groups, experts_local, tokens), "expert", split_axis=0, concat_axis=0, tiled=True
    ).reshape(experts_all, tokens)
    token_route = jnp.sum(jnp.where(chosen, returned.astype(F32)[:, None, :], 0.0), axis=0).T.astype(BF16)

    every = list(range(groups))
    all_x = jnp.concatenate([xs[o] for o in every], axis=0)
    all_g = jnp.concatenate([gs[o] for o in every], axis=0)
    all_pre = jnp.concatenate([pre_grads[o] for o in every], axis=0)
    all_scaled = jnp.concatenate([scaleds[o] for o in every], axis=0)
    rows = (((0,), (0,)), ((), ()))
    gate_part, up_part = [
        jnp.stack(
            [
                lax.dot_general(
                    all_x, all_pre[:, (s + e) * each:(s + e + 1) * each], rows, preferred_element_type=F32
                ).astype(BF16)
                for e in range(experts_local)
            ]
        )
        for s in (0, experts_local)
    ]
    down_part = (
        lax.dot_general(all_scaled, all_g, rows, preferred_element_type=F32)
        .astype(BF16)
        .reshape(experts_local, each, width)
    )
    return (upstream[None], token_route[None], gate_part[None], up_part[None], down_part[None])


def solution(mesh):
    in_specs = (
        P("section", "expert", None),
        P("section", "expert", None),
        P("section", "expert", None),
        P("section", "expert", None),
        P("section", "expert", None, None),
        P("section", "expert", None, None),
        P("section", "expert", None, None),
    )
    out_specs = (
        P("section", "expert", None),
        P("section", "expert", None),
        P("section", "expert", None, None),
        P("section", "expert", None, None),
        P("section", "expert", None, None),
    )
    return jax.shard_map(body, mesh=mesh, in_specs=in_specs, out_specs=out_specs, check_vma=False)
```

time: 241 us -> 155 us (0.64)
  blocking collectives: 45.6 us -> 0 us
  waiting for transfers between devices: 60.9 us -> 23.8 us
  starting transfers between devices: 14.6 us -> 47.7 us
  other arithmetic: 46 us -> 16 us
  between operations: 14.4 us -> 1.41 us
  local copies, waits for them, and re-layouts: 19.8 us -> 24.3 us
    all_to_all x2, waiting for transfers between devices: 49.5 us -> 0.01 us  [the longest x1 0.01 us: body(): lax.all_to_all(table.reshape(groups, experts_local, tokens), 'expert', sp...]
    all_gather x2 -> x0, blocking collectives: 45.6 us -> none  [the longest x1 23.1 us: body(): lax.all_gather(expert_ids[0].astype(jnp.bfloat16), 'expert', axis=0, tile...]
    another operation x4 -> x8, other arithmetic: 40.6 us -> 3.29 us  [block_backward(): jnp.stack([jnp.sum(product[:, e * each:(e + 1) * each], axis=1) for e in...]
    ppermute x0 -> x28, starting transfers between devices: none -> 24 us  [go(): return lax.ppermute(value, 'expert', pairs)]
    ppermute x0 -> x28, waiting for transfers between devices: none -> 21.4 us  [go(): return lax.ppermute(value, 'expert', pairs)]
    unnamed x29 -> x78, local copies, waits for them, and re-layouts: 4.09 us -> 15.7 us
    all_gather x2 -> x0, waiting for transfers between devices: 10 us -> none  [the longest x1 9.99 us: body(): lax.all_gather(out_grads[0], 'expert', axis=0, tiled=True)]
    convert_element_type x7 -> x0, local copies, waits for them, and re-layouts: 9.1 us -> none  [the longest x1 4.93 us: expert_backward(): input_grad = (jnp.einsum('esh,edh->esd', gate_pre_grad, w_gate, preferred...]
  transfers between devices with their start and end apart: 5 -> 32, of which waited for: 2 -> 10; matrix products, arithmetic and copies ran while one was open for 34% -> 47% of each run, Pallas kernels for 0% -> 0%
where the time goes in v1:
time: 155 us; the launch traced here: 154 us
  starting transfers between devices  47.7 us (31%)
  matrix products  40.8 us (26%)
  local copies, waits for them, and re-layouts  24.3 us (16%)
  waiting for transfers between devices  23.8 us (15%)
  other arithmetic  16 us (10%)
    ppermute x28, starting transfers between devices, go(): return lax.ppermute(value, 'expert', pairs)  24 us
    ppermute x28, waiting for transfers between devices, go(): return lax.ppermute(value, 'expert', pairs)  21.4 us
    unnamed x78, local copies, waits for them, and re-layouts  15.7 us
    ppermute x2, starting transfers between devices, shifted(): return lax.ppermute(value, axis, pairs)  13.4 us
    dot_general x8, matrix products, block_backward(): lax.dot_general(pre_grad, w_in, (((1,), (1,)), ((), ())), preferred_eleme...  10.5 us
    dot_general x4, matrix products, body(): lax.dot_general(all_x, all_pre[:, (s + e) * each:(s + e + 1) * each], row...  9.34 us
    dot_general x8, matrix products, block_backward(): lax.dot_general(g, w_down, (((1,), (1,)), ((), ())), preferred_element_ty...  9.34 us
    dot_general x8, matrix products, block_backward(): pre = jnp.dot(x, w_in, preferred_element_type=F32)  6.55 us
  transfers between devices with their start and end apart: 32, of which 10 were waited for; matrix products, arithmetic and copies ran while one was open for 47% of the time, Pallas kernels for 0%

profile of v1, /device:TPU:1, one launch (start us, length us, event | category | flops | bytes accessed | tf_op | source)
XLA Modules:
  0.0 153.9 jit_solution(7359194144730656748)
XLA Ops:
  0.6 2.1 %collective-permute-start.9 = (bf16[128,1024]{1,0:T(8,128)(2,1)}, bf16[128,1024]{1,0:T(8,128)(2,1)S(1)}, u32[]{:S(2)}, u32[]{:S(2)}) collective-permute-start(bf16[128,1024]{1,0:T(8,128)(2,1)} %bitcast.174), channel_id=1, source_target_pairs={{2,0},{4,2},{6,4},{7,6},{5,7},{3,5},{1,3},{0,1},{10,8},{12,10},{14... | collective-permute-start | bytes 786440 | tf_op jit(solution)/shard_map/ppermute | solution.py:70
  6.3 5.6 %all-to-all-start = ((bf16[8,2,128]{2,1,0:T(2,128)(2,1)}), bf16[8,2,128]{2,1,0:T(2,128)(2,1)S(1)}, u32[]{:S(2)}, u32[]{:S(2)}) async-start(bf16[8,2,128]{2,1,0:T(2,128)(2,1)} %bitcast.4), calls=%async_computation | async-start | bytes 8192 | tf_op jit(solution)/shard_map/all_to_all | solution.py:76
  12.0 1.7 %constant_dynamic-update-slice_fusion.7 = bf16[1024,1024]{1,0:T(8,128)(2,1)} fusion(bf16[1,128,1024]{2,1,0:T(8,128)(2,1)} %param.8), kind=kLoop, calls=%fused_computation.172 | loop fusion | bytes 524288
  13.6 1.7 %constant_dynamic-update-slice_fusion.31 = bf16[1024,1024]{1,0:T(8,128)(2,1)} fusion(bf16[1,128,1024]{2,1,0:T(8,128)(2,1)} %param.9), kind=kLoop, calls=%fused_computation.196 | loop fusion | bytes 524288
  17.4 2.2 %slice_bitcast_fusion.1 = (bf16[1024,384]{1,0:T(8,128)(2,1)S(1)}, bf16[1024,384]{1,0:T(8,128)(2,1)S(1)}, bf16[1024,384]{1,0:T(8,128)(2,1)S(1)}, bf16[1024,384]{1,0:T(8,128)(2,1)S(1)}) fusion(bf16[1,2,1024,384]{3,2,1,0:T(8,128)(2,1)} %param.13, bf16[1,2,1024,384]{3,2,1,0:T(8,128)(2,1)} %param.12), kind=kLoop, calls=%fused_computation.35 | loop fusion | bytes 6291456 | tf_op jit(solution)/shard_map/squeeze | solution.py:92
  26.0 2.5 %convolution_bitcast_fusion.3 = f32[128,1536]{1,0:T(8,128)S(1)} fusion(bf16[128,1024]{1,0:T(8,128)(2,1)S(1)} %collective-permute-done.9, bf16[1024,1536]{1,0:T(8,128)(2,1)} %copy-done.1), kind=kOutput, calls=%fused_computation.4 | convolution fusion | flops 402653184 | bytes 4194304 | tf_op jit(solution)/shard_map/dot_general | solution.py:34
  28.7 1.7 %constant_dynamic-update-slice_fusion.30 = bf16[1024,1024]{1,0:T(8,128)(2,1)} fusion(bf16[1024,1024]{1,0:T(8,128)(2,1)} %constant_dynamic-update-slice_fusion.31, bf16[128,1024]{1,0:T(8,128)(2,1)} %collective-permute-done), kind=kLoop, calls=%fused_computation.195 | loop fusion | bytes 524288
  31.6 2.9 %collective-permute-done.16 = bf16[128,1024]{1,0:T(8,128)(2,1)S(1)} collective-permute-done((bf16[128,1024]{1,0:T(8,128)(2,1)S(1)}, bf16[128,1024]{1,0:T(8,128)(2,1)S(1)}, u32[]{:S(2)}, u32[]{:S(2)}) %collective-permute-start.16) | collective-permute-done | bytes 262176 | tf_op jit(solution)/shard_map/ppermute | solution.py:70
  36.7 1.9 %convolution_convert_fusion.12 = bf16[128,1024]{1,0:T(8,128)(2,1)} fusion(bf16[1024,1536]{1,0:T(8,128)(2,1)S(1)} %copy-done.2, bf16[128,768]{1,0:T(8,128)(2,1)S(1)} %get-tuple-element.121, bf16[128,768]{1,0:T(8,128)(2,1)S(1)} %get-tuple-element.122), kind=kOutput, calls=%fused_computation.27 | convolution fusion | flops 403570688 | bytes 3801088 | tf_op jit(solution)/shard_map/dot_general | solution.py:53
  45.4 5.1 %collective-permute-done.17 = bf16[128,1024]{1,0:T(8,128)(2,1)S(1)} collective-permute-done((bf16[128,1024]{1,0:T(8,128)(2,1)S(1)}, bf16[128,1024]{1,0:T(8,128)(2,1)S(1)}, u32[]{:S(2)}, u32[]{:S(2)}) %collective-permute-start.17) | collective-permute-done | bytes 262176 | tf_op jit(solution)/shard_map/ppermute | solution.py:70
  51.8 2.5 %fusion.37 = (bf16[128,768]{1,0:T(8,128)(2,1)S(1)}, bf16[128,768]{1,0:T(8,128)(2,1)S(1)}, bf16[128,768]{1,0:T(8,128)(2,1)S(1)}, bf16[128,768]{1,0:T(8,128)(2,1)S...) fusion(f32[128]{0:T(128)S(1)} %get-tuple-element.172, ...), kind=kOutput, calls=%fused_computation.84 | convolution fusion | flops 205750272 | bytes 5776128 | tf_op jit(solution)/shard_map/dot_general | solution.py:36
  69.3 3.1 %collective-permute-done.7 = bf16[128,1024]{1,0:T(8,128)(2,1)S(1)} collective-permute-done((bf16[128,1024]{1,0:T(8,128)(2,1)S(1)}, bf16[128,1024]{1,0:T(8,128)(2,1)S(1)}, u32[]{:S(2)}, u32[]{:S(2)}) %collective-permute-start.7) | collective-permute-done | bytes 262176 | tf_op jit(solution)/shard_map/ppermute | solution.py:70
  73.1 1.8 %collective-permute-done.3 = bf16[128,1024]{1,0:T(8,128)(2,1)S(1)} collective-permute-done((bf16[128,1024]{1,0:T(8,128)(2,1)S(1)}, bf16[128,1024]{1,0:T(8,128)(2,1)S(1)}, u32[]{:S(2)}, u32[]{:S(2)}) %collective-permute-start.3) | collective-permute-done | bytes 262176 | tf_op jit(solution)/shard_map/ppermute | solution.py:70
  75.5 1.7 %fusion.40 = (bf16[128,768]{1,0:T(8,128)(2,1)}, bf16[128,768]{1,0:T(8,128)(2,1)S(1)}, bf16[128,768]{1,0:T(8,128)(2,1)S(1)}, bf16[128,768]{1,0:T(8,128)(2,1)S(1)}...) fusion(f32[128]{0:T(128)S(1)} %get-tuple-element.166, ...), kind=kOutput, calls=%fused_computation.87 | convolution fusion | flops 205750272 | bytes 5776128 | tf_op jit(solution)/shard_map/dot_general | solution.py:36
  78.4 1.9 %convolution_convert_fusion.5 = bf16[128,1024]{1,0:T(8,128)(2,1)} fusion(bf16[1024,1536]{1,0:T(8,128)(2,1)S(1)} %copy-done.2, bf16[128,768]{1,0:T(8,128)(2,1)S(1)} %get-tuple-element.129, bf16[128,768]{1,0:T(8,128)(2,1)S(1)} %get-tuple-element.130), kind=kOutput, calls=%fused_computation.20 | convolution fusion | flops 403570688 | bytes 3801088 | tf_op jit(solution)/shard_map/dot_general | solution.py:53
  82.0 2.5 %fusion.1 = bf16[1,1024,384]{2,1,0:T(8,128)(2,1)} fusion(bf16[1024,1024]{1,0:T(8,128)(2,1)S(1)} %constant_dynamic-update-slice_fusion, bf16[1024,1536]{1,0:T(8,128)(2,1)S(1)} %constant_dynamic-update-slice_fusion.8), kind=kOutput, calls=%fused_computation.17 | convolution fusion | flops 805699584 | bytes 3670016 | tf_op jit(solution)/shard_map/dot_general | solution.py:166
  84.5 2.2 %fusion = bf16[1,1024,384]{2,1,0:T(8,128)(2,1)} fusion(bf16[1024,1024]{1,0:T(8,128)(2,1)S(1)} %constant_dynamic-update-slice_fusion, bf16[1024,1536]{1,0:T(8,128)(2,1)S(1)} %constant_dynamic-update-slice_fusion.8), kind=kOutput, calls=%fused_computation.16 | convolution fusion | flops 805699584 | bytes 3670016 | tf_op jit(solution)/shard_map/dot_general | solution.py:166
  86.6 2.2 %fusion.3 = bf16[1,1024,384]{2,1,0:T(8,128)(2,1)} fusion(bf16[1024,1024]{1,0:T(8,128)(2,1)S(1)} %constant_dynamic-update-slice_fusion, bf16[1024,1536]{1,0:T(8,128)(2,1)S(1)} %constant_dynamic-update-slice_fusion.8), kind=kOutput, calls=%fused_computation.19 | convolution fusion | flops 805699584 | bytes 3670016 | tf_op jit(solution)/shard_map/dot_general | solution.py:166
  92.2 4.6 %all-to-all-start.1 = ((bf16[8,2,128]{2,1,0:T(2,128)(2,1)}), bf16[8,2,128]{2,1,0:T(2,128)(2,1)S(1)}, u32[]{:S(2)}, u32[]{:S(2)}) async-start(bf16[8,2,128]{2,1,0:T(2,128)(2,1)} %copy.38), calls=%async_computation.1 | async-start | bytes 8192 | tf_op jit(solution)/shard_map/all_to_all | solution.py:152
  96.8 1.6 %constant_dynamic-update-slice_fusion.19 = bf16[1024,768]{1,0:T(8,128)(2,1)} fusion(bf16[1024,768]{1,0:T(8,128)(2,1)} %copy-done.22, bf16[128,768]{1,0:T(8,128)(2,1)} %get-tuple-element.65), kind=kLoop, calls=%fused_computation.184 | loop fusion | bytes 393216
  98.4 1.6 %constant_dynamic-update-slice_fusion.18 = bf16[1024,768]{1,0:T(8,128)(2,1)} fusion(bf16[1024,768]{1,0:T(8,128)(2,1)} %constant_dynamic-update-slice_fusion.19, bf16[128,768]{1,0:T(8,128)(2,1)} %get-tuple-element.66), kind=kLoop, calls=%fused_computation.183 | loop fusion | bytes 393216
  100.1 1.6 %constant_dynamic-update-slice_fusion.17 = bf16[1024,768]{1,0:T(8,128)(2,1)} fusion(bf16[1024,768]{1,0:T(8,128)(2,1)} %constant_dynamic-update-slice_fusion.18, bf16[128,768]{1,0:T(8,128)(2,1)} %get-tuple-element.67), kind=kLoop, calls=%fused_computation.182 | loop fusion | bytes 393216
  101.7 1.6 %constant_dynamic-update-slice_fusion.16 = bf16[1024,768]{1,0:T(8,128)(2,1)} fusion(bf16[1024,768]{1,0:T(8,128)(2,1)} %constant_dynamic-update-slice_fusion.17, bf16[128,768]{1,0:T(8,128)(2,1)} %get-tuple-element.68), kind=kLoop, calls=%fused_computation.181 | loop fusion | bytes 393216 | tf_op jit(solution)/shard_map/concatenate | solution.py:161
  106.2 4.7 %convolution_convert_fusion = bf16[768,1024]{1,0:T(8,128)(2,1)} fusion(bf16[1024,768]{1,0:T(8,128)(2,1)S(1)} %copy-done.23, bf16[1024,1024]{1,0:T(8,128)(2,1)} %constant_dynamic-update-slice_fusion.24), kind=kOutput, calls=%fused_computation.9 | convolution fusion | flops 1611399168 | bytes 5242880 | tf_op jit(solution)/shard_map/dot_general | solution.py:175
  111.0 2.5 %fusion.2 = bf16[1,1024,384]{2,1,0:T(8,128)(2,1)S(1)} fusion(bf16[1024,1024]{1,0:T(8,128)(2,1)S(1)} %copy-done.21, bf16[1024,1536]{1,0:T(8,128)(2,1)} %copy-done.18), kind=kOutput, calls=%fused_computation.18 | convolution fusion | flops 805699584 | bytes 3670016 | tf_op jit(solution)/shard_map/dot_general | solution.py:166
  115.1 2.2 %collective-permute-done.8 = bf16[64,1024]{1,0:T(8,128)(2,1)S(1)} collective-permute-done((bf16[64,1024]{1,0:T(8,128)(2,1)S(1)}, bf16[64,1024]{1,0:T(8,128)(2,1)S(1)}, u32[]{:S(2)}, u32[]{:S(2)}) %collective-permute-start.8) | collective-permute-done | bytes 131104 | tf_op jit(solution)/shard_map/ppermute | solution.py:70
  125.0 1.7 %collective-permute-done.27 = bf16[64,1024]{1,0:T(8,128)(2,1)S(1)} collective-permute-done((bf16[64,1024]{1,0:T(8,128)(2,1)S(1)}, bf16[64,1024]{1,0:T(8,128)(2,1)S(1)}, u32[]{:S(2)}, u32[]{:S(2)}) %collective-permute-start.27) | collective-permute-done | bytes 131104 | tf_op jit(solution)/shard_map/ppermute | solution.py:70
  127.0 1.7 %collective-permute-done.23 = bf16[64,1024]{1,0:T(8,128)(2,1)S(1)} collective-permute-done((bf16[64,1024]{1,0:T(8,128)(2,1)S(1)}, bf16[64,1024]{1,0:T(8,128)(2,1)S(1)}, u32[]{:S(2)}, u32[]{:S(2)}) %collective-permute-start.23) | collective-permute-done | bytes 131104 | tf_op jit(solution)/shard_map/ppermute | solution.py:70
  133.0 2.3 %collective-permute-done.28 = bf16[64,1024]{1,0:T(8,128)(2,1)S(1)} collective-permute-done((bf16[64,1024]{1,0:T(8,128)(2,1)S(1)}, bf16[64,1024]{1,0:T(8,128)(2,1)S(1)}, u32[]{:S(2)}, u32[]{:S(2)}) %collective-permute-start.28) | collective-permute-done | bytes 131104 | tf_op jit(solution)/shard_map/ppermute | solution.py:70
  135.4 11.5 %collective-permute-start.29 = (bf16[64,1024]{1,0:T(8,128)(2,1)S(1)}, bf16[64,1024]{1,0:T(8,128)(2,1)S(1)}, u32[]{:S(2)}, u32[]{:S(2)}) collective-permute-start(bf16[64,1024]{1,0:T(8,128)(2,1)S(1)} %get-tuple-element.138), channel_id=1, source_target_pairs={{8,0},{16,8},{24,16},{9,1},{17,9},{25,17},{10,2},{18,10},{26,18},{... | collective-permute-start | bytes 393224 | tf_op jit(solution)/shard_map/ppermute | solution.py:28
  146.9 1.9 %collective-permute-start.21 = (bf16[64,1024]{1,0:T(8,128)(2,1)S(1)}, bf16[64,1024]{1,0:T(8,128)(2,1)S(1)}, u32[]{:S(2)}, u32[]{:S(2)}) collective-permute-start(bf16[64,1024]{1,0:T(8,128)(2,1)S(1)} %get-tuple-element.137), channel_id=1, source_target_pairs={{8,0},{16,8},{24,16},{9,1},{17,9},{25,17},{10,2},{18,10},{26,18},{... | collective-permute-start | bytes 393224 | tf_op jit(solution)/shard_map/ppermute | solution.py:28
  150.8 2.4 %collective-permute-done.21 = bf16[64,1024]{1,0:T(8,128)(2,1)S(1)} collective-permute-done((bf16[64,1024]{1,0:T(8,128)(2,1)S(1)}, bf16[64,1024]{1,0:T(8,128)(2,1)S(1)}, u32[]{:S(2)}, u32[]{:S(2)}) %collective-permute-start.21) | collective-permute-done | bytes 131104 | tf_op jit(solution)/shard_map/ppermute | solution.py:28
  (206 shorter events, 65.3 us)
Async XLA Ops:
  0.6 25.1 %collective-permute-start.9 = (bf16[128,1024]{1,0:T(8,128)(2,1)}, bf16[128,1024]{1,0:T(8,128)(2,1)S(1)}, u32[]{:S(2)}, u32[]{:S(2)}) collective-permute-start(bf16[128,1024]{1,0:T(8,128)(2,1)} %bitcast.174), channel_id=1, source_target_pairs={{2,0},{4,2},{6,4},{7,6},{5,7},{3,5},{1,3},{0,1},{10,8},{12,10},{14... | collective-permute-start | bytes 786440 | tf_op jit(solution)/shard_map/ppermute | solution.py:70
  2.7 20.3 %collective-permute-start.4 = (bf16[128,1024]{1,0:T(8,128)(2,1)}, bf16[128,1024]{1,0:T(8,128)(2,1)S(1)}, u32[]{:S(2)}, u32[]{:S(2)}) collective-permute-start(bf16[128,1024]{1,0:T(8,128)(2,1)} %bitcast.175), channel_id=1, source_target_pairs={{0,2},{2,4},{4,6},{6,7},{7,5},{5,3},{3,1},{1,0},{8,10},{10,12},{12... | collective-permute-start | bytes 786440 | tf_op jit(solution)/shard_map/ppermute | solution.py:70
  2.9 21.6 %collective-permute-start.15 = (bf16[128,1024]{1,0:T(8,128)(2,1)}, bf16[128,1024]{1,0:T(8,128)(2,1)S(1)}, u32[]{:S(2)}, u32[]{:S(2)}) collective-permute-start(bf16[128,1024]{1,0:T(8,128)(2,1)} %bitcast.176), channel_id=1, source_target_pairs={{0,2},{2,4},{4,6},{6,7},{7,5},{5,3},{3,1},{1,0},{8,10},{10,12},{12... | collective-permute-start | bytes 786440 | tf_op jit(solution)/shard_map/ppermute | solution.py:70
  4.3 24.2 %collective-permute-start = (bf16[128,1024]{1,0:T(8,128)(2,1)}, bf16[128,1024]{1,0:T(8,128)(2,1)}, u32[]{:S(2)}, u32[]{:S(2)}) collective-permute-start(bf16[128,1024]{1,0:T(8,128)(2,1)} %bitcast.177), channel_id=1, source_target_pairs={{2,0},{4,2},{6,4},{7,6},{5,7},{3,5},{1,3},{0,1},{10,8},{12,10},{14... | collective-permute-start | bytes 786440 | tf_op jit(solution)/shard_map/ppermute | solution.py:70
  6.3 16.5 %all-to-all-start = ((bf16[8,2,128]{2,1,0:T(2,128)(2,1)}), bf16[8,2,128]{2,1,0:T(2,128)(2,1)S(1)}, u32[]{:S(2)}, u32[]{:S(2)}) async-start(bf16[8,2,128]{2,1,0:T(2,128)(2,1)} %bitcast.4), calls=%async_computation | async-start | bytes 8192 | tf_op jit(solution)/shard_map/all_to_all | solution.py:76
  23.0 8.0 %collective-permute-start.5 = (bf16[128,1024]{1,0:T(8,128)(2,1)S(1)}, bf16[128,1024]{1,0:T(8,128)(2,1)S(1)}, u32[]{:S(2)}, u32[]{:S(2)}) collective-permute-start(bf16[128,1024]{1,0:T(8,128)(2,1)S(1)} %collective-permute-done.4), channel_id=1, source_target_pairs={{0,2},{2,4},{4,6},{6,7},{7,5},{5,3},{3,1},{1,0},{8,10},{10,12},{12... | collective-permute-start | bytes 786440 | tf_op jit(solution)/shard_map/ppermute | solution.py:70
  24.5 9.9 %collective-permute-start.16 = (bf16[128,1024]{1,0:T(8,128)(2,1)S(1)}, bf16[128,1024]{1,0:T(8,128)(2,1)S(1)}, u32[]{:S(2)}, u32[]{:S(2)}) collective-permute-start(bf16[128,1024]{1,0:T(8,128)(2,1)S(1)} %collective-permute-done.15), channel_id=1, source_target_pairs={{0,2},{2,4},{4,6},{6,7},{7,5},{5,3},{3,1},{1,0},{8,10},{10,12},{12... | collective-permute-start | bytes 786440 | tf_op jit(solution)/shard_map/ppermute | solution.py:70
  25.7 14.5 %collective-permute-start.10 = (bf16[128,1024]{1,0:T(8,128)(2,1)S(1)}, bf16[128,1024]{1,0:T(8,128)(2,1)S(1)}, u32[]{:S(2)}, u32[]{:S(2)}) collective-permute-start(bf16[128,1024]{1,0:T(8,128)(2,1)S(1)} %collective-permute-done.9), channel_id=1, source_target_pairs={{2,0},{4,2},{6,4},{7,6},{5,7},{3,5},{1,3},{0,1},{10,8},{12,10},{14... | collective-permute-start | bytes 786440 | tf_op jit(solution)/shard_map/ppermute | solution.py:70
  28.5 13.8 %collective-permute-start.1 = (bf16[128,1024]{1,0:T(8,128)(2,1)}, bf16[128,1024]{1,0:T(8,128)(2,1)S(1)}, u32[]{:S(2)}, u32[]{:S(2)}) collective-permute-start(bf16[128,1024]{1,0:T(8,128)(2,1)} %collective-permute-done), channel_id=1, source_target_pairs={{2,0},{4,2},{6,4},{7,6},{5,7},{3,5},{1,3},{0,1},{10,8},{12,10},{14... | collective-permute-start | bytes 786440 | tf_op jit(solution)/shard_map/ppermute | solution.py:70
  38.8 6.0 %collective-permute-start.6 = (bf16[128,1024]{1,0:T(8,128)(2,1)S(1)}, bf16[128,1024]{1,0:T(8,128)(2,1)S(1)}, u32[]{:S(2)}, u32[]{:S(2)}) collective-permute-start(bf16[128,1024]{1,0:T(8,128)(2,1)S(1)} %collective-permute-done.5), channel_id=1, source_target_pairs={{0,2},{2,4},{4,6},{6,7},{7,5},{5,3},{3,1},{1,0},{8,10},{10,12},{12... | collective-permute-start | bytes 786440 | tf_op jit(solution)/shard_map/ppermute | solution.py:70
  41.9 9.3 %collective-permute-start.11 = (bf16[128,1024]{1,0:T(8,128)(2,1)S(1)}, bf16[128,1024]{1,0:T(8,128)(2,1)S(1)}, u32[]{:S(2)}, u32[]{:S(2)}) collective-permute-start(bf16[128,1024]{1,0:T(8,128)(2,1)S(1)} %collective-permute-done.10), channel_id=1, source_target_pairs={{2,0},{4,2},{6,4},{7,6},{5,7},{3,5},{1,3},{0,1},{10,8},{12,10},{14... | collective-permute-start | bytes 786440 | tf_op jit(solution)/shard_map/ppermute | solution.py:70
  42.3 13.2 %collective-permute-start.2 = (bf16[128,1024]{1,0:T(8,128)(2,1)S(1)}, bf16[128,1024]{1,0:T(8,128)(2,1)S(1)}, u32[]{:S(2)}, u32[]{:S(2)}) collective-permute-start(bf16[128,1024]{1,0:T(8,128)(2,1)S(1)} %collective-permute-done.1), channel_id=1, source_target_pairs={{2,0},{4,2},{6,4},{7,6},{5,7},{3,5},{1,3},{0,1},{10,8},{12,10},{14... | collective-permute-start | bytes 786440 | tf_op jit(solution)/shard_map/ppermute | solution.py:70
  44.3 6.3 %collective-permute-start.17 = (bf16[128,1024]{1,0:T(8,128)(2,1)S(1)}, bf16[128,1024]{1,0:T(8,128)(2,1)S(1)}, u32[]{:S(2)}, u32[]{:S(2)}) collective-permute-start(bf16[128,1024]{1,0:T(8,128)(2,1)S(1)} %collective-permute-done.16), channel_id=1, source_target_pairs={{0,2},{2,4},{4,6},{6,7},{7,5},{5,3},{3,1},{1,0},{8,10},{10,12},{12... | collective-permute-start | bytes 786440 | tf_op jit(solution)/shard_map/ppermute | solution.py:70
  62.1 56.8 %collective-permute-start.18 = (bf16[64,1024]{1,0:T(8,128)(2,1)}, bf16[64,1024]{1,0:T(8,128)(2,1)}, u32[]{:S(2)}, u32[]{:S(2)}) collective-permute-start(bf16[64,1024]{1,0:T(8,128)(2,1)} %slice.285), channel_id=1, source_target_pairs={{2,0},{4,2},{6,4},{7,6},{5,7},{3,5},{1,3},{0,1},{10,8},{12,10},{14... | collective-permute-start | bytes 393224 | tf_op jit(solution)/shard_map/ppermute | solution.py:70
  65.6 55.8 %collective-permute-start.22 = (bf16[64,1024]{1,0:T(8,128)(2,1)}, bf16[64,1024]{1,0:T(8,128)(2,1)}, u32[]{:S(2)}, u32[]{:S(2)}) collective-permute-start(bf16[64,1024]{1,0:T(8,128)(2,1)} %slice.301), channel_id=1, source_target_pairs={{0,2},{2,4},{4,6},{6,7},{7,5},{5,3},{3,1},{1,0},{8,10},{10,12},{12... | collective-permute-start | bytes 393224 | tf_op jit(solution)/shard_map/ppermute | solution.py:70
  66.7 5.7 %collective-permute-start.7 = (bf16[128,1024]{1,0:T(8,128)(2,1)S(1)}, bf16[128,1024]{1,0:T(8,128)(2,1)S(1)}, u32[]{:S(2)}, u32[]{:S(2)}) collective-permute-start(bf16[128,1024]{1,0:T(8,128)(2,1)S(1)} %collective-permute-done.6), channel_id=1, source_target_pairs={{0,2},{2,4},{4,6},{6,7},{7,5},{5,3},{3,1},{1,0},{8,10},{10,12},{12... | collective-permute-start | bytes 786440 | tf_op jit(solution)/shard_map/ppermute | solution.py:70
  69.0 5.9 %collective-permute-start.3 = (bf16[128,1024]{1,0:T(8,128)(2,1)S(1)}, bf16[128,1024]{1,0:T(8,128)(2,1)S(1)}, u32[]{:S(2)}, u32[]{:S(2)}) collective-permute-start(bf16[128,1024]{1,0:T(8,128)(2,1)S(1)} %collective-permute-done.2), channel_id=1, source_target_pairs={{2,0},{4,2},{6,4},{7,6},{5,7},{3,5},{1,3},{0,1},{10,8},{12,10},{14... | collective-permute-start | bytes 786440 | tf_op jit(solution)/shard_map/ppermute | solution.py:70
  89.6 25.5 %collective-permute-start.25 = (bf16[64,1024]{1,0:T(8,128)(2,1)}, bf16[64,1024]{1,0:T(8,128)(2,1)S(1)}, u32[]{:S(2)}, u32[]{:S(2)}) collective-permute-start(bf16[64,1024]{1,0:T(8,128)(2,1)} %get-tuple-element.144), channel_id=1, source_target_pairs={{2,0},{4,2},{6,4},{7,6},{5,7},{3,5},{1,3},{0,1},{10,8},{12,10},{14... | collective-permute-start | bytes 393224 | tf_op jit(solution)/shard_map/ppermute | solution.py:70
  92.2 58.0 %all-to-all-start.1 = ((bf16[8,2,128]{2,1,0:T(2,128)(2,1)}), bf16[8,2,128]{2,1,0:T(2,128)(2,1)S(1)}, u32[]{:S(2)}, u32[]{:S(2)}) async-start(bf16[8,2,128]{2,1,0:T(2,128)(2,1)} %copy.38), calls=%async_computation.1 | async-start | bytes 8192 | tf_op jit(solution)/shard_map/all_to_all | solution.py:152
  113.5 3.9 %collective-permute-start.8 = (bf16[64,1024]{1,0:T(8,128)(2,1)S(1)}, bf16[64,1024]{1,0:T(8,128)(2,1)S(1)}, u32[]{:S(2)}, u32[]{:S(2)}) collective-permute-start(bf16[64,1024]{1,0:T(8,128)(2,1)S(1)} %copy-done.17), channel_id=1, source_target_pairs={{0,2},{2,4},{4,6},{6,7},{7,5},{5,3},{3,1},{1,0},{8,10},{10,12},{12... | collective-permute-start | bytes 393224 | tf_op jit(solution)/shard_map/ppermute | solution.py:70
  115.1 3.9 %collective-permute-start.26 = (bf16[64,1024]{1,0:T(8,128)(2,1)S(1)}, bf16[64,1024]{1,0:T(8,128)(2,1)S(1)}, u32[]{:S(2)}, u32[]{:S(2)}) collective-permute-start(bf16[64,1024]{1,0:T(8,128)(2,1)S(1)} %add_convert_fusion.3), channel_id=1, source_target_pairs={{2,0},{4,2},{6,4},{7,6},{5,7},{3,5},{1,3},{0,1},{10,8},{12,10},{14... | collective-permute-start | bytes 393224 | tf_op jit(solution)/shard_map/ppermute | solution.py:70
  117.4 4.0 %collective-permute-start.12 = (bf16[64,1024]{1,0:T(8,128)(2,1)S(1)}, bf16[64,1024]{1,0:T(8,128)(2,1)S(1)}, u32[]{:S(2)}, u32[]{:S(2)}) collective-permute-start(bf16[64,1024]{1,0:T(8,128)(2,1)S(1)} %add_convert_fusion.11), channel_id=1, source_target_pairs={{0,2},{2,4},{4,6},{6,7},{7,5},{5,3},{3,1},{1,0},{8,10},{10,12},{12... | collective-permute-start | bytes 393224 | tf_op jit(solution)/shard_map/ppermute | solution.py:70
  119.9 5.1 %collective-permute-start.19 = (bf16[64,1024]{1,0:T(8,128)(2,1)S(1)}, bf16[64,1024]{1,0:T(8,128)(2,1)S(1)}, u32[]{:S(2)}, u32[]{:S(2)}) collective-permute-start(bf16[64,1024]{1,0:T(8,128)(2,1)S(1)} %get-tuple-element.147), channel_id=1, source_target_pairs={{2,0},{4,2},{6,4},{7,6},{5,7},{3,5},{1,3},{0,1},{10,8},{12,10},{14... | collective-permute-start | bytes 393224 | tf_op jit(solution)/shard_map/ppermute | solution.py:70
  120.0 6.7 %collective-permute-start.27 = (bf16[64,1024]{1,0:T(8,128)(2,1)S(1)}, bf16[64,1024]{1,0:T(8,128)(2,1)S(1)}, u32[]{:S(2)}, u32[]{:S(2)}) collective-permute-start(bf16[64,1024]{1,0:T(8,128)(2,1)S(1)} %get-tuple-element.148), channel_id=1, source_target_pairs={{2,0},{4,2},{6,4},{7,6},{5,7},{3,5},{1,3},{0,1},{10,8},{12,10},{14... | collective-permute-start | bytes 393224 | tf_op jit(solution)/shard_map/ppermute | solution.py:70
  122.4 4.6 %collective-permute-start.13 = (bf16[64,1024]{1,0:T(8,128)(2,1)S(1)}, bf16[64,1024]{1,0:T(8,128)(2,1)S(1)}, u32[]{:S(2)}, u32[]{:S(2)}) collective-permute-start(bf16[64,1024]{1,0:T(8,128)(2,1)S(1)} %get-tuple-element.141), channel_id=1, source_target_pairs={{0,2},{2,4},{4,6},{6,7},{7,5},{5,3},{3,1},{1,0},{8,10},{10,12},{12... | collective-permute-start | bytes 393224 | tf_op jit(solution)/shard_map/ppermute | solution.py:70
  123.8 5.0 %collective-permute-start.23 = (bf16[64,1024]{1,0:T(8,128)(2,1)S(1)}, bf16[64,1024]{1,0:T(8,128)(2,1)S(1)}, u32[]{:S(2)}, u32[]{:S(2)}) collective-permute-start(bf16[64,1024]{1,0:T(8,128)(2,1)S(1)} %get-tuple-element.142), channel_id=1, source_target_pairs={{0,2},{2,4},{4,6},{6,7},{7,5},{5,3},{3,1},{1,0},{8,10},{10,12},{12... | collective-permute-start | bytes 393224 | tf_op jit(solution)/shard_map/ppermute | solution.py:70
  126.8 5.8 %collective-permute-start.20 = (bf16[64,1024]{1,0:T(8,128)(2,1)S(1)}, bf16[64,1024]{1,0:T(8,128)(2,1)S(1)}, u32[]{:S(2)}, u32[]{:S(2)}) collective-permute-start(bf16[64,1024]{1,0:T(8,128)(2,1)S(1)} %get-tuple-element.145), channel_id=1, source_target_pairs={{2,0},{4,2},{6,4},{7,6},{5,7},{3,5},{1,3},{0,1},{10,8},{12,10},{14... | collective-permute-start | bytes 393224 | tf_op jit(solution)/shard_map/ppermute | solution.py:70
  128.8 4.2 %collective-permute-start.14 = (bf16[64,1024]{1,0:T(8,128)(2,1)S(1)}, bf16[64,1024]{1,0:T(8,128)(2,1)S(1)}, u32[]{:S(2)}, u32[]{:S(2)}) collective-permute-start(bf16[64,1024]{1,0:T(8,128)(2,1)S(1)} %get-tuple-element.139), channel_id=1, source_target_pairs={{0,2},{2,4},{4,6},{6,7},{7,5},{5,3},{3,1},{1,0},{8,10},{10,12},{12... | collective-permute-start | bytes 393224 | tf_op jit(solution)/shard_map/ppermute | solution.py:70
  129.7 5.5 %collective-permute-start.28 = (bf16[64,1024]{1,0:T(8,128)(2,1)S(1)}, bf16[64,1024]{1,0:T(8,128)(2,1)S(1)}, u32[]{:S(2)}, u32[]{:S(2)}) collective-permute-start(bf16[64,1024]{1,0:T(8,128)(2,1)S(1)} %get-tuple-element.146), channel_id=1, source_target_pairs={{2,0},{4,2},{6,4},{7,6},{5,7},{3,5},{1,3},{0,1},{10,8},{12,10},{14... | collective-permute-start | bytes 393224 | tf_op jit(solution)/shard_map/ppermute | solution.py:70
  130.3 4.9 %collective-permute-start.24 = (bf16[64,1024]{1,0:T(8,128)(2,1)S(1)}, bf16[64,1024]{1,0:T(8,128)(2,1)S(1)}, u32[]{:S(2)}, u32[]{:S(2)}) collective-permute-start(bf16[64,1024]{1,0:T(8,128)(2,1)S(1)} %get-tuple-element.140), channel_id=1, source_target_pairs={{0,2},{2,4},{4,6},{6,7},{7,5},{5,3},{3,1},{1,0},{8,10},{10,12},{12... | collective-permute-start | bytes 393224 | tf_op jit(solution)/shard_map/ppermute | solution.py:70
  135.4 15.4 %collective-permute-start.29 = (bf16[64,1024]{1,0:T(8,128)(2,1)S(1)}, bf16[64,1024]{1,0:T(8,128)(2,1)S(1)}, u32[]{:S(2)}, u32[]{:S(2)}) collective-permute-start(bf16[64,1024]{1,0:T(8,128)(2,1)S(1)} %get-tuple-element.138), channel_id=1, source_target_pairs={{8,0},{16,8},{24,16},{9,1},{17,9},{25,17},{10,2},{18,10},{26,18},{... | collective-permute-start | bytes 393224 | tf_op jit(solution)/shard_map/ppermute | solution.py:28
  146.9 6.3 %collective-permute-start.21 = (bf16[64,1024]{1,0:T(8,128)(2,1)S(1)}, bf16[64,1024]{1,0:T(8,128)(2,1)S(1)}, u32[]{:S(2)}, u32[]{:S(2)}) collective-permute-start(bf16[64,1024]{1,0:T(8,128)(2,1)S(1)} %get-tuple-element.137), channel_id=1, source_target_pairs={{8,0},{16,8},{24,16},{9,1},{17,9},{25,17},{10,2},{18,10},{26,18},{... | collective-permute-start | bytes 393224 | tf_op jit(solution)/shard_map/ppermute | solution.py:28
  (25 other events, 216.5 us)

commit v2 on v1

v2 whole, which is shorter than its diff:
```python
import functools

import jax
import jax.numpy as jnp
from jax import lax
from jax.experimental import pallas as pl
from jax.experimental.pallas import tpu as pltpu
from jax.sharding import PartitionSpec as P

F32 = jnp.float32
BF16 = jnp.bfloat16
LAST = (((1,), (1,)), ((), ()))
ROWS = (((0,), (0,)), ((), ()))


def ring_order(size):
    columns = 1
    while (2 * columns) ** 2 <= size and size % (2 * columns) == 0:
        columns *= 2
    rows = size // columns
    if columns == 1:
        return list(range(size))
    cells = [(0, 0)]
    for column in range(columns):
        span = range(1, rows) if column % 2 == 0 else range(rows - 1, 0, -1)
        cells += [(row, column) for row in span]
    cells += [(0, column) for column in range(columns - 1, 0, -1)]
    return [row * columns + column for row, column in cells]


def shifted(value, axis, by):
    size = lax.axis_size(axis)
    pairs = [(i, i + by) for i in range(size) if 0 <= i + by < size]
    return lax.ppermute(value, axis, pairs)


def block_kernel(count, tokens, cut, *refs):
    first_ref, refs = refs[0], refs[1:]
    xs, gs, routes = refs[:count], refs[count:2 * count], refs[2 * count:3 * count]
    w_gate, w_up, w_down = refs[3 * count:3 * count + 3]
    outs = refs[3 * count + 3:]
    parts, (gate_out, up_out, scaled), (acc, table) = outs[:2 * count], outs[2 * count:-2], outs[-2:]
    experts_all = table.shape[1]
    e = pl.program_id(0)
    x = jnp.concatenate([ref[...] for ref in xs], axis=0)
    g = jnp.concatenate([ref[...] for ref in gs], axis=0)
    route = jnp.concatenate(
        [jnp.broadcast_to(ref[0], (tokens, tokens)).T[:, :1] for ref in routes], axis=0
    )
    gate = jnp.dot(x, w_gate[0], preferred_element_type=F32)
    up = jnp.dot(x, w_up[0], preferred_element_type=F32)
    back = lax.dot_general(g, w_down[0], LAST, preferred_element_type=F32)
    sig = jax.nn.sigmoid(gate)
    silu = gate * sig
    active = (silu * up).astype(BF16).astype(F32)
    scaled[0] = (route * active).astype(BF16)
    product = active * back
    coarse = product.astype(BF16)
    fine = (product - coarse.astype(F32)).astype(BF16)
    ones = jnp.ones((experts_all, product.shape[1]), BF16)
    row_grad = lax.dot_general(ones, coarse, LAST, preferred_element_type=F32) + lax.dot_general(
        ones, fine, LAST, preferred_element_type=F32
    )
    own_row = lax.broadcasted_iota(jnp.int32, (experts_all, tokens), 0) == first_ref[0] + e
    grad = route * back
    gate_grad = (grad * up * sig * (1.0 + gate * (1.0 - sig))).astype(BF16)
    up_grad = (grad * silu).astype(BF16)
    gate_out[0] = gate_grad
    up_out[0] = up_grad
    part = lax.dot_general(gate_grad, w_gate[0], LAST, preferred_element_type=F32) + lax.dot_general(
        up_grad, w_up[0], LAST, preferred_element_type=F32
    )

    @pl.when(e == 0)
    def _():
        acc[...] = part
        table[...] = jnp.zeros(table.shape, F32)

    @pl.when(e > 0)
    def _():
        acc[...] += part

    for i in range(count):
        table[i] = jnp.where(own_row, row_grad[:, i * tokens:(i + 1) * tokens], table[i])

    @pl.when(e == pl.num_programs(0) - 1)
    def _():
        for i in range(count):
            parts[2 * i][:cut, :] = acc[i * tokens:i * tokens + cut, :].astype(BF16)
            parts[2 * i][cut:, :] = jnp.zeros((experts_all, acc.shape[1]), BF16)
            parts[2 * i][cut:, :tokens] = table[i].astype(BF16)
            parts[2 * i + 1][...] = acc[i * tokens + cut:(i + 1) * tokens, :].astype(BF16)


def block_backward(first, xs, gs, routes, offsets, experts_all, w_gate, w_up, w_down):
    count = len(xs)
    tokens, width = xs[0].shape
    experts, _, each = w_gate.shape
    rows = count * tokens
    cut = tokens // 2

    def whole(shape):
        return pl.BlockSpec(shape, lambda e: (0,) * len(shape))

    def own(shape):
        return pl.BlockSpec((1,) + shape, lambda e: (e, 0, 0))

    def route_of(o):
        return pl.BlockSpec((1, 1, tokens), lambda e: (o * experts + e, 0, 0))

    halves = [(cut + experts_all, width), (tokens - cut, width)] * count
    outs = pl.pallas_call(
        functools.partial(block_kernel, count, tokens, cut),
        grid=(experts,),
        in_specs=[pl.BlockSpec(memory_space=pltpu.SMEM)]
        + [whole((tokens, width))] * (2 * count)
        + [route_of(o) for o in offsets]
        + [own((width, each)), own((width, each)), own((each, width))],
        out_specs=[whole(shape) for shape in halves]
        + [own((rows, each))] * 3,
        out_shape=[jax.ShapeDtypeStruct(shape, BF16) for shape in halves]
        + [jax.ShapeDtypeStruct((experts, rows, each), BF16)] * 3,
        scratch_shapes=[pltpu.VMEM((rows, width), F32), pltpu.VMEM((count, experts_all, tokens), F32)],
        compiler_params=pltpu.CompilerParams(dimension_semantics=("arbitrary",)),
        cost_estimate=pl.CostEstimate(
            flops=10 * rows * width * each * experts,
            bytes_accessed=6 * experts * width * each + 6 * rows * width,
            transcendentals=rows * each * experts,
        ),
        name="experts_block",
    )(first, *xs, *gs, *([routes] * count), w_gate, w_up, w_down)
    return outs[:2 * count], outs[2 * count:]


def update_kernel(talls, thins, parts, turned, *refs):
    tall_refs, thin_refs = refs[:talls], refs[talls:talls + thins * parts]
    outs, scratch = refs[talls + thins * parts:-1], refs[-1]

    @pl.when(pl.program_id(0) == 0)
    def _():
        tall = jnp.concatenate([ref[...] for ref in tall_refs], axis=0)
        scratch[...] = tall.T if turned else tall

    for p in range(parts):
        thin = jnp.concatenate([ref[0] for ref in thin_refs[p * thins:(p + 1) * thins]], axis=0)
        if turned:
            outs[p][0] = jnp.dot(scratch[...], thin, preferred_element_type=F32).astype(BF16)
        else:
            outs[p][0] = lax.dot_general(thin, scratch[...], ROWS, preferred_element_type=F32).astype(BF16)


def update(tall, thins, turned):
    count, parts = len(tall), len(thins)
    experts, _, each = thins[0][0].shape
    width = tall[0].shape[1]
    rows = sum(t.shape[0] for t in tall)
    shape = (width, each) if turned else (each, width)
    thin = [t for group in thins for t in group]
    return pl.pallas_call(
        functools.partial(update_kernel, count, len(thins[0]), parts, turned),
        grid=(experts,),
        in_specs=[pl.BlockSpec(t.shape, lambda e: (0, 0)) for t in tall]
        + [pl.BlockSpec((1,) + t.shape[1:], lambda e: (e, 0, 0)) for t in thin],
        out_specs=[pl.BlockSpec((1,) + shape, lambda e: (e, 0, 0))] * parts,
        out_shape=[jax.ShapeDtypeStruct((experts,) + shape, BF16)] * parts,
        scratch_shapes=[pltpu.VMEM((width, rows) if turned else (rows, width), BF16)],
        compiler_params=pltpu.CompilerParams(dimension_semantics=("arbitrary",)),
        cost_estimate=pl.CostEstimate(
            flops=2 * rows * width * each * experts * parts,
            bytes_accessed=2 * (rows * width + parts * experts * each * (rows + width)),
            transcendentals=0,
        ),
        name="weight_update",
    )(*tall, *thin)


def body(inputs, out_grads, expert_ids, route_levels, w_gate, w_up, w_down):
    x0, g0 = inputs[0], out_grads[0]
    ids = expert_ids[0]
    tokens, _ = x0.shape
    experts_local, _, _ = w_gate.shape[1:]
    groups = lax.axis_size("expert")
    experts_all = experts_local * groups
    half = groups // 2
    ring = ring_order(groups)
    fwd = [(ring[p], ring[(p + 1) % groups]) for p in range(groups)]
    bwd = [(b, a) for a, b in fwd]

    def go(value, pairs):
        return lax.ppermute(value, "expert", pairs)

    levels = route_levels[0].astype(F32) / 256.0
    catalog = jnp.arange(experts_all, dtype=jnp.int32)
    chosen = ids.T[None, :, :] == catalog[:, None, None]
    table = jnp.sum(jnp.where(chosen, levels.T[None], 0.0), axis=1).astype(BF16)
    received = lax.all_to_all(
        table.reshape(groups, experts_local, tokens), "expert", split_axis=0, concat_axis=0, tiled=True
    )
    ring_arr = jnp.array(ring, jnp.int32)
    me = lax.axis_index("expert")
    place = jnp.sum(jnp.where(ring_arr == me, jnp.arange(groups), 0))
    seat = jnp.sum(
        jnp.where(ring_arr[None, :] == jnp.arange(groups)[:, None], jnp.arange(groups)[None, :], 0), axis=1
    )
    turn = (
        jnp.mod(seat[None, :] - place, groups) == jnp.arange(groups)[:, None]
    ).astype(BF16)
    routes = jnp.dot(turn, received.reshape(groups, -1), preferred_element_type=F32)
    routes = routes.reshape(groups * experts_local, 1, tokens)
    first = (me * experts_local).astype(jnp.int32).reshape(1)

    xs, gs = {0: x0}, {0: g0}
    xf = xb = x0
    gf = gb = g0
    for hop in range(1, half + 1):
        xf = go(xf, fwd)
        gb = go(gb, bwd)
        xs[groups - hop], gs[hop] = xf, gb
        if hop < half:
            gf = go(gf, fwd)
            xb = go(xb, bwd)
            gs[groups - hop], xs[hop] = gf, xb

    low, high, tall_x, tall_g, thin = {}, {}, [], [], []
    for hop in range(half + 1):
        offsets = list(dict.fromkeys([hop, (groups - hop) % groups]))
        parts, grads = block_backward(
            first, [xs[o] for o in offsets], [gs[o] for o in offsets], routes, offsets, experts_all,
            w_gate[0], w_up[0], w_down[0],
        )
        for i, o in enumerate(offsets):
            low[o], high[o] = parts[2 * i], parts[2 * i + 1]
            tall_x.append(xs[o])
            tall_g.append(gs[o])
        thin.append(grads)

    def chain(pieces, pairs, offsets):
        carried = []
        for o in offsets:
            piece = pieces[o]
            if carried:
                piece = (carried[-1].astype(F32) + piece.astype(F32)).astype(BF16)
            carried.append(go(piece, pairs))
        return carried

    longer = list(range(half, 0, -1))
    forward_high = chain(high, fwd, longer[1:])
    backward_low = chain(low, bwd, [groups - o for o in longer[1:]])
    forward_low = chain(low, fwd, longer)
    backward_high = chain(high, bwd, [groups - o for o in longer])

    def total(own, one, two):
        return (own.astype(F32) + one[-1].astype(F32) + two[-1].astype(F32)).astype(BF16)

    low_total = total(low[0], forward_low, backward_low)
    cut = tokens // 2
    upstream = jnp.concatenate(
        [
            shifted(low_total[:cut], "section", -1),
            shifted(total(high[0], forward_high, backward_high), "section", -1),
        ],
        axis=0,
    )
    returned = low_total[cut:, :tokens].astype(F32)
    token_route = jnp.sum(jnp.where(chosen, returned[:, None, :], 0.0), axis=0).T.astype(BF16)

    gate_part, up_part = update(tall_x, [[t[0] for t in thin], [t[1] for t in thin]], True)
    (down_part,) = update(tall_g, [[t[2] for t in thin]], False)
    return (upstream[None], token_route[None], gate_part[None], up_part[None], down_part[None])


def solution(mesh):
    in_specs = (
        P("section", "expert", None),
        P("section", "expert", None),
        P("section", "expert", None),
        P("section", "expert", None),
        P("section", "expert", None, None),
        P("section", "expert", None, None),
        P("section", "expert", None, None),
    )
    out_specs = (
        P("section", "expert", None),
        P("section", "expert", None),
        P("section", "expert", None, None),
        P("section", "expert", None, None),
        P("section", "expert", None, None),
    )

    return jax.shard_map(body, mesh=mesh, in_specs=in_specs, out_specs=out_specs, check_vma=False)
```

time: 155 us -> 127 us (0.82)
  Pallas kernels: 0 us -> 48.5 us
  matrix products: 40.8 us -> 0.12 us
  local copies, waits for them, and re-layouts: 24.3 us -> 3.69 us
  other arithmetic: 16 us -> 8.4 us
  waiting for transfers between devices: 23.8 us -> 20 us
  starting transfers between devices: 47.7 us -> 44.6 us
    pallas_call x0 -> x7, Pallas kernels: none -> 48.5 us  [the longest x5 34.7 us: block_backward(): pl.pallas_call(functools.partial(block_kernel, count, tokens, cut), grid=...]
    dot_general x30 -> x0, matrix products: 40.7 us -> none  [the longest x8 10.5 us: block_backward(): lax.dot_general(pre_grad, w_in, (((1,), (1,)), ((), ())), preferred_eleme...]
    unnamed x78 -> x56, local copies, waits for them, and re-layouts: 15.7 us -> 3.07 us
    ppermute x28, waiting for transfers between devices: 21.4 us -> 16 us  [go(): return lax.ppermute(value, 'expert', pairs)]
    all_to_all x1 -> x0, starting transfers between devices: 4.6 us -> none  [body(): lax.all_to_all(back_table.reshape(groups, experts_local, tokens), 'expert...]
    concatenate x5 -> x0, local copies, waits for them, and re-layouts: 3.77 us -> none  [the longest x1 1.62 us: body(): all_scaled = jnp.concatenate([scaleds[o] for o in every], axis=0)]
    ppermute x2, starting transfers between devices: 13.4 us -> 16.9 us  [shifted(): return lax.ppermute(value, axis, pairs)]
    another operation x8 -> x0, other arithmetic: 3.29 us -> none  [block_backward(): jnp.stack([jnp.sum(product[:, e * each:(e + 1) * each], axis=1) for e in...]
  transfers between devices with their start and end apart: 32 -> 31, of which waited for: 10 -> 11; matrix products, arithmetic and copies ran while one was open for 47% -> 7% of each run, Pallas kernels for 0% -> 32%
where the time goes in v2:
time: 127 us; the launch traced here: 126 us
  Pallas kernels  48.5 us (38%)
  starting transfers between devices  44.6 us (35%)
  waiting for transfers between devices  20 us (16%)
  other arithmetic  8.4 us (7%)
  local copies, waits for them, and re-layouts  3.69 us (3%)
    pallas_call x5, Pallas kernels, block_backward(): pl.pallas_call(functools.partial(block_kernel, count, tokens, cut), grid=...  34.7 us
    ppermute x28, starting transfers between devices, go(): return lax.ppermute(value, 'expert', pairs)  22 us
    ppermute x2, starting transfers between devices, shifted(): return lax.ppermute(value, axis, pairs)  16.9 us
    ppermute x28, waiting for transfers between devices, go(): return lax.ppermute(value, 'expert', pairs)  16 us
    pallas_call x2, Pallas kernels, update(): pl.pallas_call(functools.partial(update_kernel, count, len(thins[0]), par...  13.8 us
    all_to_all x1, starting transfers between devices, body(): lax.all_to_all(table.reshape(groups, experts_local, tokens), 'expert', sp...  5.63 us
    ppermute x2, waiting for transfers between devices, shifted(): return lax.ppermute(value, axis, pairs)  3.49 us
    unnamed x56, local copies, waits for them, and re-layouts  3.07 us
  transfers between devices with their start and end apart: 31, of which 11 were waited for; matrix products, arithmetic and copies ran while one was open for 7% of the time, Pallas kernels for 32%

profile of v2, /device:TPU:1, one launch (start us, length us, event | category | flops | bytes accessed | tf_op | source)
XLA Modules:
  0.0 126.3 jit_solution(2442008073256801421)
XLA Ops:
  0.6 2.1 %collective-permute-start.9 = (bf16[128,1024]{1,0:T(8,128)(2,1)}, bf16[128,1024]{1,0:T(8,128)(2,1)S(1)}, u32[]{:S(2)}, u32[]{:S(2)}) collective-permute-start(bf16[128,1024]{1,0:T(8,128)(2,1)} %bitcast.43), channel_id=1, source_target_pairs={{2,0},{4,2},{6,4},{7,6},{5,7},{3,5},{1,3},{0,1},{10,8},{12,10},{14... | collective-permute-start | bytes 786440 | tf_op jit(solution)/shard_map/ppermute | solution.py:190
  2.9 1.4 %collective-permute-start.12 = (bf16[128,1024]{1,0:T(8,128)(2,1)}, bf16[128,1024]{1,0:T(8,128)(2,1)S(1)}, u32[]{:S(2)}, u32[]{:S(2)}) collective-permute-start(bf16[128,1024]{1,0:T(8,128)(2,1)} %bitcast.47), channel_id=1, source_target_pairs={{0,2},{2,4},{4,6},{6,7},{7,5},{5,3},{3,1},{1,0},{8,10},{10,12},{12... | collective-permute-start | bytes 786440 | tf_op jit(solution)/shard_map/ppermute | solution.py:190
  5.0 1.3 %select_reduce_fusion.1 = bf16[16,128]{1,0:T(8,128)(2,1)} fusion(f32[8,128]{1,0:T(8,128)S(1)} %multiply_bitcast_fusion, s32[8,128]{1,0:T(8,128)} %bitcast.51), kind=kLoop, calls=%fused_computation.14 | loop fusion | flops 47104 | bytes 12288 | tf_op jit(solution)/shard_map/reduce_sum | solution.py:195
  6.3 5.6 %all-to-all-start = ((bf16[8,2,128]{2,1,0:T(2,128)(2,1)}), bf16[8,2,128]{2,1,0:T(2,128)(2,1)S(1)}, u32[]{:S(2)}, u32[]{:S(2)}) async-start(bf16[8,2,128]{2,1,0:T(2,128)(2,1)} %bitcast.7), calls=%async_computation | async-start | bytes 8192 | tf_op jit(solution)/shard_map/all_to_all | solution.py:196
  12.7 1.3 %fusion.4 = s32[]{:T(128)} fusion(s32[8]{0:T(128)} %constant.29.clone, s32[]{:T(128)S(6)} %axis_index.12), kind=kLoop, calls=%fused_computation.30 | loop fusion | flops 23 | bytes 40 | tf_op jit(solution)/shard_map/reduce_sum | solution.py:201
  14.0 1.5 %collective-permute-start.10 = (bf16[128,1024]{1,0:T(8,128)(2,1)S(1)}, bf16[128,1024]{1,0:T(8,128)(2,1)S(1)}, u32[]{:S(2)}, u32[]{:S(2)}) collective-permute-start(bf16[128,1024]{1,0:T(8,128)(2,1)S(1)} %collective-permute-done.9.refs_1_), channel_id=1, source_target_pairs={{2,0},{4,2},{6,4},{7,6},{5,7},{3,5},{1,3},{0,1},{10,8},{12,10},{14... | collective-permute-start | bytes 786440 | tf_op jit(solution)/shard_map/ppermute | solution.py:190
  15.6 1.4 %collective-permute-start.13 = (bf16[128,1024]{1,0:T(8,128)(2,1)S(1)}, bf16[128,1024]{1,0:T(8,128)(2,1)S(1)}, u32[]{:S(2)}, u32[]{:S(2)}) collective-permute-start(bf16[128,1024]{1,0:T(8,128)(2,1)S(1)} %collective-permute-done.12.refs_4_.refs_2_), channel_id=1, source_target_pairs={{0,2},{2,4},{4,6},{6,7},{7,5},{5,3},{3,1},{1,0},{8,10},{10,12},{12... | collective-permute-start | bytes 786440 | tf_op jit(solution)/shard_map/ppermute | solution.py:190
  19.9 1.1 collective-permute-start.11
  21.4 5.0 %collective-permute-done.13.refs_4_ = bf16[128,1024]{1,0:T(8,128)(2,1)S(1)} collective-permute-done((bf16[128,1024]{1,0:T(8,128)(2,1)S(1)}, bf16[128,1024]{1,0:T(8,128)(2,1)S(1)}, u32[]{:S(2)}, u32[]{:S(2)}) %collective-permute-start.13) | collective-permute-done | bytes 262176 | tf_op jit(solution)/shard_map/ppermute | solution.py:190
  26.7 1.2 collective-permute-start.6
  27.9 5.9 %experts_block.5 = (bf16[80,1024]{1,0:T(8,128)(2,1)}, bf16[64,1024]{1,0:T(8,128)(2,1)}, bf16[2,128,384]{2,1,0:T(8,128)(2,1)}, bf16[2,128,384]{2,1,0:T(8,128)(2,1)}, bf16[2,128,384]{2,1,0:T(8,128)(2,1)}) custom-call(s32[1]{0:T(128)} %bitcast.refs_0_, bf16[128,1024]{1,0:T(8,128)(2,1)} %bitcast.45, bf16[128,1024]{1,0:T(8,128)(2,1)} %bitcast.49, ...), custom_call_target="tpu_custom_call" | custom-call | flops 1006632960 | bytes 5505024 | tf_op jit(solution)/shard_map/experts_block/pallas_call | solution.py:112
  33.8 7.7 %experts_block.9 = (bf16[80,1024]{1,0:T(8,128)(2,1)}, bf16[64,1024]{1,0:T(8,128)(2,1)}, bf16[80,1024]{1,0:T(8,128)(2,1)}, bf16[64,1024]{1,0:T(8,128)(2,1)}, bf16...) custom-call(s32[1]{0:T(128)} %bitcast.refs_0_, bf16[128,1024]{1,0:T(8,128)(2,1)} %copy-done.15, ...), custom_call_target="tpu_custom_call" | custom-call | flops 2013265920 | bytes 6291456 | tf_op jit(solution)/shard_map/experts_block/pallas_call | solution.py:112
  43.1 7.6 %experts_block.7 = (bf16[80,1024]{1,0:T(8,128)(2,1)}, bf16[64,1024]{1,0:T(8,128)(2,1)}, bf16[80,1024]{1,0:T(8,128)(2,1)}, bf16[64,1024]{1,0:T(8,128)(2,1)}, bf16...) custom-call(s32[1]{0:T(128)} %bitcast.refs_0_, bf16[128,1024]{1,0:T(8,128)(2,1)} %copy-done.22, ...), custom_call_target="tpu_custom_call" | custom-call | flops 2013265920 | bytes 6291456 | tf_op jit(solution)/shard_map/experts_block/pallas_call | solution.py:112
  51.1 7.7 %experts_block.8 = (bf16[80,1024]{1,0:T(8,128)(2,1)}, bf16[64,1024]{1,0:T(8,128)(2,1)}, bf16[80,1024]{1,0:T(8,128)(2,1)}, bf16[64,1024]{1,0:T(8,128)(2,1)}, bf16...) custom-call(s32[1]{0:T(128)} %bitcast.refs_0_, bf16[128,1024]{1,0:T(8,128)(2,1)} %copy-done.18, ...), custom_call_target="tpu_custom_call" | custom-call | flops 2013265920 | bytes 6291456 | tf_op jit(solution)/shard_map/experts_block/pallas_call | solution.py:112
  58.8 1.2 collective-permute-start.18
  60.3 1.2 collective-permute-start.7
  64.0 1.2 collective-permute-start.19
  65.2 1.4 %collective-permute-done.23 = bf16[64,1024]{1,0:T(8,128)(2,1)S(1)} collective-permute-done((bf16[64,1024]{1,0:T(8,128)(2,1)S(1)}, bf16[64,1024]{1,0:T(8,128)(2,1)S(1)}, u32[]{:S(2)}, u32[]{:S(2)}) %collective-permute-start.23) | collective-permute-done | bytes 131104 | tf_op jit(solution)/shard_map/ppermute | solution.py:190
  68.5 5.9 %experts_block.6 = (bf16[80,1024]{1,0:T(8,128)(2,1)}, bf16[64,1024]{1,0:T(8,128)(2,1)}, bf16[2,128,384]{2,1,0:T(8,128)(2,1)}, bf16[2,128,384]{2,1,0:T(8,128)(2,1)}, bf16[2,128,384]{2,1,0:T(8,128)(2,1)}) custom-call(s32[1]{0:T(128)} %bitcast.refs_0_, bf16[128,1024]{1,0:T(8,128)(2,1)} %copy-done.1, bf16[128,1024]{1,0:T(8,128)(2,1)} %copy-done, ...), custom_call_target="tpu_custom_call" | custom-call | flops 1006632960 | bytes 5505024 | tf_op jit(solution)/shard_map/experts_block/pallas_call | solution.py:112
  74.3 1.2 collective-permute-start.25
  75.8 8.6 %weight_update.2 = (bf16[2,1024,384]{2,1,0:T(8,128)(2,1)}, bf16[2,1024,384]{2,1,0:T(8,128)(2,1)}) custom-call(bf16[128,1024]{1,0:T(8,128)(2,1)} %bitcast.46, bf16[128,1024]{1,0:T(8,128)(2,1)} %copy-done.15, bf16[128,1024]{1,0:T(8,128)(2,1)} %copy-done.16, bf16[128,1024]{1,0:T(8,128)(2,1)} %copy-done.18, bf16[128,1024]{1,0:T(8,128)(2,1)} %copy-done.20, ...), custom_call_target="tpu_custom_call" | custom-call | flops 3221225472 | bytes 8388608 | tf_op jit(solution)/shard_map/weight_update/pallas_call | solution.py:159
  84.5 5.2 %weight_update.3 = bf16[2,384,1024]{2,1,0:T(8,128)(2,1)} custom-call(bf16[128,1024]{1,0:T(8,128)(2,1)} %bitcast.50, bf16[128,1024]{1,0:T(8,128)(2,1)} %copy-done.14, bf16[128,1024]{1,0:T(8,128)(2,1)} %copy-done.13, bf16[128,1024]{1,0:T(8,128)(2,1)} %copy-done.19, bf16[128,1024]{1,0:T(8,128)(2,1)} %copy-done.17, bf16[128,1024]{1,0:T(8,128)(2,1)} %copy-done.23, ...), custom_call_target="tpu_custom_call" | custom-call | flops 1610612736 | bytes 5242880 | tf_op jit(solution)/shard_map/weight_update/pallas_call | solution.py:159
  89.8 1.2 collective-permute-start.20
  91.1 1.2 collective-permute-start.26
  92.7 2.7 %collective-permute-done.26 = bf16[64,1024]{1,0:T(8,128)(2,1)S(1)} collective-permute-done((bf16[64,1024]{1,0:T(8,128)(2,1)S(1)}, bf16[64,1024]{1,0:T(8,128)(2,1)S(1)}, u32[]{:S(2)}, u32[]{:S(2)}) %collective-permute-start.26) | collective-permute-done | bytes 131104 | tf_op jit(solution)/shard_map/ppermute | solution.py:190
  95.5 1.2 collective-permute-start.27
  97.1 2.2 %collective-permute-done.27 = bf16[64,1024]{1,0:T(8,128)(2,1)S(1)} collective-permute-done((bf16[64,1024]{1,0:T(8,128)(2,1)S(1)}, bf16[64,1024]{1,0:T(8,128)(2,1)S(1)}, u32[]{:S(2)}, u32[]{:S(2)}) %collective-permute-start.27) | collective-permute-done | bytes 131104 | tf_op jit(solution)/shard_map/ppermute | solution.py:190
  99.4 1.2 collective-permute-start.28
  101.4 3.0 %collective-permute-done.28 = bf16[64,1024]{1,0:T(8,128)(2,1)S(1)} collective-permute-done((bf16[64,1024]{1,0:T(8,128)(2,1)S(1)}, bf16[64,1024]{1,0:T(8,128)(2,1)S(1)}, u32[]{:S(2)}, u32[]{:S(2)}) %collective-permute-start.28) | collective-permute-done | bytes 131104 | tf_op jit(solution)/shard_map/ppermute | solution.py:190
  104.5 14.7 %collective-permute-start.29 = (bf16[64,1024]{1,0:T(8,128)(2,1)S(1)}, bf16[64,1024]{1,0:T(8,128)(2,1)S(1)}, u32[]{:S(2)}, u32[]{:S(2)}) collective-permute-start(bf16[64,1024]{1,0:T(8,128)(2,1)S(1)} %add_convert_fusion.6), channel_id=1, source_target_pairs={{8,0},{16,8},{24,16},{9,1},{17,9},{25,17},{10,2},{18,10},{26,18},{... | collective-permute-start | bytes 393224 | tf_op jit(solution)/shard_map/ppermute | solution.py:34
  119.3 2.2 %collective-permute-start.21 = (bf16[64,1024]{1,0:T(8,128)(2,1)S(1)}, bf16[64,1024]{1,0:T(8,128)(2,1)S(1)}, u32[]{:S(2)}, u32[]{:S(2)}) collective-permute-start(bf16[64,1024]{1,0:T(8,128)(2,1)S(1)} %slice.8), channel_id=1, source_target_pairs={{8,0},{16,8},{24,16},{9,1},{17,9},{25,17},{10,2},{18,10},{26,18},{... | collective-permute-start | bytes 393224 | tf_op jit(solution)/shard_map/ppermute | solution.py:34
  123.0 2.6 %collective-permute-done.21 = bf16[64,1024]{1,0:T(8,128)(2,1)S(1)} collective-permute-done((bf16[64,1024]{1,0:T(8,128)(2,1)S(1)}, bf16[64,1024]{1,0:T(8,128)(2,1)S(1)}, u32[]{:S(2)}, u32[]{:S(2)}) %collective-permute-start.21) | collective-permute-done | bytes 131104 | tf_op jit(solution)/shard_map/ppermute | solution.py:34
  (116 shorter events, 16.2 us)
Async XLA Ops:
  0.6 13.4 %collective-permute-start.9 = (bf16[128,1024]{1,0:T(8,128)(2,1)}, bf16[128,1024]{1,0:T(8,128)(2,1)S(1)}, u32[]{:S(2)}, u32[]{:S(2)}) collective-permute-start(bf16[128,1024]{1,0:T(8,128)(2,1)} %bitcast.43), channel_id=1, source_target_pairs={{2,0},{4,2},{6,4},{7,6},{5,7},{3,5},{1,3},{0,1},{10,8},{12,10},{14... | collective-permute-start | bytes 786440 | tf_op jit(solution)/shard_map/ppermute | solution.py:190
  2.7 12.8 %collective-permute-start = (bf16[128,1024]{1,0:T(8,128)(2,1)}, bf16[128,1024]{1,0:T(8,128)(2,1)S(1)}, u32[]{:S(2)}, u32[]{:S(2)}) collective-permute-start(bf16[128,1024]{1,0:T(8,128)(2,1)} %bitcast.44), channel_id=1, source_target_pairs={{0,2},{2,4},{4,6},{6,7},{7,5},{5,3},{3,1},{1,0},{8,10},{10,12},{12... | collective-permute-start | bytes 786440 | tf_op jit(solution)/shard_map/ppermute | solution.py:190
  2.9 12.7 %collective-permute-start.12 = (bf16[128,1024]{1,0:T(8,128)(2,1)}, bf16[128,1024]{1,0:T(8,128)(2,1)S(1)}, u32[]{:S(2)}, u32[]{:S(2)}) collective-permute-start(bf16[128,1024]{1,0:T(8,128)(2,1)} %bitcast.47), channel_id=1, source_target_pairs={{0,2},{2,4},{4,6},{6,7},{7,5},{5,3},{3,1},{1,0},{8,10},{10,12},{12... | collective-permute-start | bytes 786440 | tf_op jit(solution)/shard_map/ppermute | solution.py:190
  4.3 12.7 %collective-permute-start.4 = (bf16[128,1024]{1,0:T(8,128)(2,1)}, bf16[128,1024]{1,0:T(8,128)(2,1)S(1)}, u32[]{:S(2)}, u32[]{:S(2)}) collective-permute-start(bf16[128,1024]{1,0:T(8,128)(2,1)} %bitcast.48), channel_id=1, source_target_pairs={{2,0},{4,2},{6,4},{7,6},{5,7},{3,5},{1,3},{0,1},{10,8},{12,10},{14... | collective-permute-start | bytes 786440 | tf_op jit(solution)/shard_map/ppermute | solution.py:190
  6.3 11.9 %all-to-all-start = ((bf16[8,2,128]{2,1,0:T(2,128)(2,1)}), bf16[8,2,128]{2,1,0:T(2,128)(2,1)S(1)}, u32[]{:S(2)}, u32[]{:S(2)}) async-start(bf16[8,2,128]{2,1,0:T(2,128)(2,1)} %bitcast.7), calls=%async_computation | async-start | bytes 8192 | tf_op jit(solution)/shard_map/all_to_all | solution.py:196
  14.0 5.9 %collective-permute-start.10 = (bf16[128,1024]{1,0:T(8,128)(2,1)S(1)}, bf16[128,1024]{1,0:T(8,128)(2,1)S(1)}, u32[]{:S(2)}, u32[]{:S(2)}) collective-permute-start(bf16[128,1024]{1,0:T(8,128)(2,1)S(1)} %collective-permute-done.9.refs_1_), channel_id=1, source_target_pairs={{2,0},{4,2},{6,4},{7,6},{5,7},{3,5},{1,3},{0,1},{10,8},{12,10},{14... | collective-permute-start | bytes 786440 | tf_op jit(solution)/shard_map/ppermute | solution.py:190
  15.5 5.5 %collective-permute-start.1 = (bf16[128,1024]{1,0:T(8,128)(2,1)S(1)}, bf16[128,1024]{1,0:T(8,128)(2,1)S(1)}, u32[]{:S(2)}, u32[]{:S(2)}) collective-permute-start(bf16[128,1024]{1,0:T(8,128)(2,1)S(1)} %collective-permute-done.refs_2_), channel_id=1, source_target_pairs={{0,2},{2,4},{4,6},{6,7},{7,5},{5,3},{3,1},{1,0},{8,10},{10,12},{12... | collective-permute-start | bytes 786440 | tf_op jit(solution)/shard_map/ppermute | solution.py:190
  15.6 10.8 %collective-permute-start.13 = (bf16[128,1024]{1,0:T(8,128)(2,1)S(1)}, bf16[128,1024]{1,0:T(8,128)(2,1)S(1)}, u32[]{:S(2)}, u32[]{:S(2)}) collective-permute-start(bf16[128,1024]{1,0:T(8,128)(2,1)S(1)} %collective-permute-done.12.refs_4_.refs_2_), channel_id=1, source_target_pairs={{0,2},{2,4},{4,6},{6,7},{7,5},{5,3},{3,1},{1,0},{8,10},{10,12},{12... | collective-permute-start | bytes 786440 | tf_op jit(solution)/shard_map/ppermute | solution.py:190
  17.0 9.7 %collective-permute-start.5 = (bf16[128,1024]{1,0:T(8,128)(2,1)S(1)}, bf16[128,1024]{1,0:T(8,128)(2,1)S(1)}, u32[]{:S(2)}, u32[]{:S(2)}) collective-permute-start(bf16[128,1024]{1,0:T(8,128)(2,1)S(1)} %collective-permute-done.4.refs_3_.refs_1_), channel_id=1, source_target_pairs={{2,0},{4,2},{6,4},{7,6},{5,7},{3,5},{1,3},{0,1},{10,8},{12,10},{14... | collective-permute-start | bytes 786440 | tf_op jit(solution)/shard_map/ppermute | solution.py:190
  19.9 21.6 %collective-permute-start.11 = (bf16[128,1024]{1,0:T(8,128)(2,1)S(1)}, bf16[128,1024]{1,0:T(8,128)(2,1)S(1)}, u32[]{:S(2)}, u32[]{:S(2)}) collective-permute-start(bf16[128,1024]{1,0:T(8,128)(2,1)S(1)} %collective-permute-done.10.refs_1_.refs_3_), channel_id=1, source_target_pairs={{2,0},{4,2},{6,4},{7,6},{5,7},{3,5},{1,3},{0,1},{10,8},{12,10},{14... | collective-permute-start | bytes 786440 | tf_op jit(solution)/shard_map/ppermute | solution.py:190
  21.0 20.4 %collective-permute-start.2 = (bf16[128,1024]{1,0:T(8,128)(2,1)S(1)}, bf16[128,1024]{1,0:T(8,128)(2,1)S(1)}, u32[]{:S(2)}, u32[]{:S(2)}) collective-permute-start(bf16[128,1024]{1,0:T(8,128)(2,1)S(1)} %collective-permute-done.1.refs_2_.refs_4_), channel_id=1, source_target_pairs={{0,2},{2,4},{4,6},{6,7},{7,5},{5,3},{3,1},{1,0},{8,10},{10,12},{12... | collective-permute-start | bytes 786440 | tf_op jit(solution)/shard_map/ppermute | solution.py:190
  26.4 15.1 %collective-permute-start.14 = (bf16[128,1024]{1,0:T(8,128)(2,1)S(1)}, bf16[128,1024]{1,0:T(8,128)(2,1)S(1)}, u32[]{:S(2)}, u32[]{:S(2)}) collective-permute-start(bf16[128,1024]{1,0:T(8,128)(2,1)S(1)} %collective-permute-done.13.refs_4_), channel_id=1, source_target_pairs={{0,2},{2,4},{4,6},{6,7},{7,5},{5,3},{3,1},{1,0},{8,10},{10,12},{12... | collective-permute-start | bytes 786440 | tf_op jit(solution)/shard_map/ppermute | solution.py:190
  26.7 14.8 %collective-permute-start.6 = (bf16[128,1024]{1,0:T(8,128)(2,1)S(1)}, bf16[128,1024]{1,0:T(8,128)(2,1)S(1)}, u32[]{:S(2)}, u32[]{:S(2)}) collective-permute-start(bf16[128,1024]{1,0:T(8,128)(2,1)S(1)} %collective-permute-done.5.refs_3_), channel_id=1, source_target_pairs={{2,0},{4,2},{6,4},{7,6},{5,7},{3,5},{1,3},{0,1},{10,8},{12,10},{14... | collective-permute-start | bytes 786440 | tf_op jit(solution)/shard_map/ppermute | solution.py:190
  50.8 10.7 %collective-permute-start.22 = (bf16[64,1024]{1,0:T(8,128)(2,1)}, bf16[64,1024]{1,0:T(8,128)(2,1)S(1)}, u32[]{:S(2)}, u32[]{:S(2)}) collective-permute-start(bf16[64,1024]{1,0:T(8,128)(2,1)} %get-tuple-element.47), channel_id=1, source_target_pairs={{0,2},{2,4},{4,6},{6,7},{7,5},{5,3},{3,1},{1,0},{8,10},{10,12},{12... | collective-permute-start | bytes 393224 | tf_op jit(solution)/shard_map/ppermute | solution.py:190
  58.8 4.2 %collective-permute-start.18 = (bf16[80,1024]{1,0:T(8,128)(2,1)S(1)}, bf16[80,1024]{1,0:T(8,128)(2,1)S(1)}, u32[]{:S(2)}, u32[]{:S(2)}) collective-permute-start(bf16[80,1024]{1,0:T(8,128)(2,1)S(1)} %copy-done.27), channel_id=1, source_target_pairs={{2,0},{4,2},{6,4},{7,6},{5,7},{3,5},{1,3},{0,1},{10,8},{12,10},{14... | collective-permute-start | bytes 491528 | tf_op jit(solution)/shard_map/ppermute | solution.py:190
  60.0 7.0 %collective-permute-start.3 = (bf16[128,1024]{1,0:T(8,128)(2,1)S(1)}, bf16[128,1024]{1,0:T(8,128)(2,1)S(1)}, u32[]{:S(2)}, u32[]{:S(2)}) collective-permute-start(bf16[128,1024]{1,0:T(8,128)(2,1)S(1)} %copy-done.26), channel_id=1, source_target_pairs={{0,2},{2,4},{4,6},{6,7},{7,5},{5,3},{3,1},{1,0},{8,10},{10,12},{12... | collective-permute-start | bytes 786440 | tf_op jit(solution)/shard_map/ppermute | solution.py:190
  60.3 6.7 %collective-permute-start.7 = (bf16[128,1024]{1,0:T(8,128)(2,1)S(1)}, bf16[128,1024]{1,0:T(8,128)(2,1)S(1)}, u32[]{:S(2)}, u32[]{:S(2)}) collective-permute-start(bf16[128,1024]{1,0:T(8,128)(2,1)S(1)} %copy-done.24), channel_id=1, source_target_pairs={{2,0},{4,2},{6,4},{7,6},{5,7},{3,5},{1,3},{0,1},{10,8},{12,10},{14... | collective-permute-start | bytes 786440 | tf_op jit(solution)/shard_map/ppermute | solution.py:190
  62.4 4.2 %collective-permute-start.23 = (bf16[64,1024]{1,0:T(8,128)(2,1)S(1)}, bf16[64,1024]{1,0:T(8,128)(2,1)S(1)}, u32[]{:S(2)}, u32[]{:S(2)}) collective-permute-start(bf16[64,1024]{1,0:T(8,128)(2,1)S(1)} %add_convert_fusion.11), channel_id=1, source_target_pairs={{0,2},{2,4},{4,6},{6,7},{7,5},{5,3},{3,1},{1,0},{8,10},{10,12},{12... | collective-permute-start | bytes 393224 | tf_op jit(solution)/shard_map/ppermute | solution.py:190
  64.0 25.8 %collective-permute-start.19 = (bf16[80,1024]{1,0:T(8,128)(2,1)S(1)}, bf16[80,1024]{1,0:T(8,128)(2,1)S(1)}, u32[]{:S(2)}, u32[]{:S(2)}) collective-permute-start(bf16[80,1024]{1,0:T(8,128)(2,1)S(1)} %add_convert_fusion.2), channel_id=1, source_target_pairs={{2,0},{4,2},{6,4},{7,6},{5,7},{3,5},{1,3},{0,1},{10,8},{12,10},{14... | collective-permute-start | bytes 491528 | tf_op jit(solution)/shard_map/ppermute | solution.py:190
  66.7 34.7 %collective-permute-start.24 = (bf16[64,1024]{1,0:T(8,128)(2,1)S(1)}, bf16[64,1024]{1,0:T(8,128)(2,1)S(1)}, u32[]{:S(2)}, u32[]{:S(2)}) collective-permute-start(bf16[64,1024]{1,0:T(8,128)(2,1)S(1)} %add_convert_fusion.10), channel_id=1, source_target_pairs={{0,2},{2,4},{4,6},{6,7},{7,5},{5,3},{3,1},{1,0},{8,10},{10,12},{12... | collective-permute-start | bytes 393224 | tf_op jit(solution)/shard_map/ppermute | solution.py:190
  74.3 16.7 %collective-permute-start.25 = (bf16[64,1024]{1,0:T(8,128)(2,1)}, bf16[64,1024]{1,0:T(8,128)(2,1)S(1)}, u32[]{:S(2)}, u32[]{:S(2)}) collective-permute-start(bf16[64,1024]{1,0:T(8,128)(2,1)} %get-tuple-element.50), channel_id=1, source_target_pairs={{2,0},{4,2},{6,4},{7,6},{5,7},{3,5},{1,3},{0,1},{10,8},{12,10},{14... | collective-permute-start | bytes 393224 | tf_op jit(solution)/shard_map/ppermute | solution.py:190
  75.5 16.8 %collective-permute-start.8 = (bf16[80,1024]{1,0:T(8,128)(2,1)}, bf16[80,1024]{1,0:T(8,128)(2,1)S(1)}, u32[]{:S(2)}, u32[]{:S(2)}) collective-permute-start(bf16[80,1024]{1,0:T(8,128)(2,1)} %get-tuple-element.39), channel_id=1, source_target_pairs={{0,2},{2,4},{4,6},{6,7},{7,5},{5,3},{3,1},{1,0},{8,10},{10,12},{12... | collective-permute-start | bytes 491528 | tf_op jit(solution)/shard_map/ppermute | solution.py:190
  89.8 29.4 %collective-permute-start.20 = (bf16[80,1024]{1,0:T(8,128)(2,1)S(1)}, bf16[80,1024]{1,0:T(8,128)(2,1)S(1)}, u32[]{:S(2)}, u32[]{:S(2)}) collective-permute-start(bf16[80,1024]{1,0:T(8,128)(2,1)S(1)} %add_convert_fusion.1), channel_id=1, source_target_pairs={{2,0},{4,2},{6,4},{7,6},{5,7},{3,5},{1,3},{0,1},{10,8},{12,10},{14... | collective-permute-start | bytes 491528 | tf_op jit(solution)/shard_map/ppermute | solution.py:190
  91.0 28.2 %copy-start.2 = (bf16[80,1024]{1,0:T(8,128)(2,1)S(1)}, bf16[80,1024]{1,0:T(8,128)(2,1)}, u32[]{:S(2)}) copy-start(bf16[80,1024]{1,0:T(8,128)(2,1)} %get-tuple-element.38) | copy-start | bytes 491524
  91.1 4.4 %collective-permute-start.26 = (bf16[64,1024]{1,0:T(8,128)(2,1)S(1)}, bf16[64,1024]{1,0:T(8,128)(2,1)S(1)}, u32[]{:S(2)}, u32[]{:S(2)}) collective-permute-start(bf16[64,1024]{1,0:T(8,128)(2,1)S(1)} %add_convert_fusion.9), channel_id=1, source_target_pairs={{2,0},{4,2},{6,4},{7,6},{5,7},{3,5},{1,3},{0,1},{10,8},{12,10},{14... | collective-permute-start | bytes 393224 | tf_op jit(solution)/shard_map/ppermute | solution.py:190
  92.4 4.3 %collective-permute-start.15 = (bf16[80,1024]{1,0:T(8,128)(2,1)S(1)}, bf16[80,1024]{1,0:T(8,128)(2,1)S(1)}, u32[]{:S(2)}, u32[]{:S(2)}) collective-permute-start(bf16[80,1024]{1,0:T(8,128)(2,1)S(1)} %add_convert_fusion.5), channel_id=1, source_target_pairs={{0,2},{2,4},{4,6},{6,7},{7,5},{5,3},{3,1},{1,0},{8,10},{10,12},{12... | collective-permute-start | bytes 491528 | tf_op jit(solution)/shard_map/ppermute | solution.py:190
  95.5 3.9 %collective-permute-start.27 = (bf16[64,1024]{1,0:T(8,128)(2,1)S(1)}, bf16[64,1024]{1,0:T(8,128)(2,1)S(1)}, u32[]{:S(2)}, u32[]{:S(2)}) collective-permute-start(bf16[64,1024]{1,0:T(8,128)(2,1)S(1)} %add_convert_fusion.8), channel_id=1, source_target_pairs={{2,0},{4,2},{6,4},{7,6},{5,7},{3,5},{1,3},{0,1},{10,8},{12,10},{14... | collective-permute-start | bytes 393224 | tf_op jit(solution)/shard_map/ppermute | solution.py:190
  96.8 4.2 %collective-permute-start.16 = (bf16[80,1024]{1,0:T(8,128)(2,1)S(1)}, bf16[80,1024]{1,0:T(8,128)(2,1)S(1)}, u32[]{:S(2)}, u32[]{:S(2)}) collective-permute-start(bf16[80,1024]{1,0:T(8,128)(2,1)S(1)} %add_convert_fusion.4), channel_id=1, source_target_pairs={{0,2},{2,4},{4,6},{6,7},{7,5},{5,3},{3,1},{1,0},{8,10},{10,12},{12... | collective-permute-start | bytes 491528 | tf_op jit(solution)/shard_map/ppermute | solution.py:190
  99.4 5.0 %collective-permute-start.28 = (bf16[64,1024]{1,0:T(8,128)(2,1)S(1)}, bf16[64,1024]{1,0:T(8,128)(2,1)S(1)}, u32[]{:S(2)}, u32[]{:S(2)}) collective-permute-start(bf16[64,1024]{1,0:T(8,128)(2,1)S(1)} %add_convert_fusion.7), channel_id=1, source_target_pairs={{2,0},{4,2},{6,4},{7,6},{5,7},{3,5},{1,3},{0,1},{10,8},{12,10},{14... | collective-permute-start | bytes 393224 | tf_op jit(solution)/shard_map/ppermute | solution.py:190
  101.0 18.2 %collective-permute-start.17 = (bf16[80,1024]{1,0:T(8,128)(2,1)S(1)}, bf16[80,1024]{1,0:T(8,128)(2,1)S(1)}, u32[]{:S(2)}, u32[]{:S(2)}) collective-permute-start(bf16[80,1024]{1,0:T(8,128)(2,1)S(1)} %add_convert_fusion.3), channel_id=1, source_target_pairs={{0,2},{2,4},{4,6},{6,7},{7,5},{5,3},{3,1},{1,0},{8,10},{10,12},{12... | collective-permute-start | bytes 491528 | tf_op jit(solution)/shard_map/ppermute | solution.py:190
  104.5 18.5 %collective-permute-start.29 = (bf16[64,1024]{1,0:T(8,128)(2,1)S(1)}, bf16[64,1024]{1,0:T(8,128)(2,1)S(1)}, u32[]{:S(2)}, u32[]{:S(2)}) collective-permute-start(bf16[64,1024]{1,0:T(8,128)(2,1)S(1)} %add_convert_fusion.6), channel_id=1, source_target_pairs={{8,0},{16,8},{24,16},{9,1},{17,9},{25,17},{10,2},{18,10},{26,18},{... | collective-permute-start | bytes 393224 | tf_op jit(solution)/shard_map/ppermute | solution.py:34
  119.3 6.3 %collective-permute-start.21 = (bf16[64,1024]{1,0:T(8,128)(2,1)S(1)}, bf16[64,1024]{1,0:T(8,128)(2,1)S(1)}, u32[]{:S(2)}, u32[]{:S(2)}) collective-permute-start(bf16[64,1024]{1,0:T(8,128)(2,1)S(1)} %slice.8), channel_id=1, source_target_pairs={{8,0},{16,8},{24,16},{9,1},{17,9},{25,17},{10,2},{18,10},{26,18},{... | collective-permute-start | bytes 393224 | tf_op jit(solution)/shard_map/ppermute | solution.py:34
  (27 other events, 260.6 us)
